TPU v7x, 32 devices: a whole 2x2x4 slice. The times are simulated.
32 devices in a mesh: ctx: 4 (over x, core), exp: 8 (over z, y).
Axes of the slice: x: 2, y: 2, z: 4, core: 2. Of those that a mesh axis runs over, the one named last changes fastest.
Arguments:
- q_nope: bfloat16 [128, 128, 512], P('ctx', 'exp'), may hold values from -72 to 72
- q_rope: bfloat16 [128, 8192], P('ctx', 'exp'), may hold values from -6 to 6
- cache_keys: bfloat16 [576, 512], P(None, 'ctx'), may hold values from -6 to 6
- fresh_keys: bfloat16 [576, 128], P(None, 'ctx'), may hold values from -6 to 6
- block_order: int32 [8], replicated, may hold values from 0 to 7, each once
- w_uv: bfloat16 [128, 512, 128], P('exp'), may hold values from -0.25 to 0.25
- w_out: bfloat16 [16384, 7168], P('exp', 'ctx'), may hold values from -0.046875 to 0.046875
- residual: bfloat16 [128, 7168], P(('ctx', 'exp')), may hold values from -6 to 6
- norm_gain: float32 [7168], replicated, may hold values from 0.5 to 1.5
- router_weight: bfloat16 [7168, 16], replicated, may hold values from -0.0625 to 0.0625
- expert_ids: int32 [128, 8], P(('ctx', 'exp')), may hold values from 0 to 15, all different within a row; in each aligned block of 4 rows (0 to 3, 4 to 7, ...) at most 3 rows name the same one
- w_gate: bfloat16 [16, 7168, 2048], P('exp', None, 'ctx'), may hold values from -0.0625 to 0.0625
- w_up: bfloat16 [16, 7168, 2048], P('exp', None, 'ctx'), may hold values from -0.0625 to 0.0625
- w_down: bfloat16 [16, 2048, 7168], P('exp', 'ctx'), may hold values from -0.125 to 0.125
Outputs:
- layer_out: bfloat16 [128, 7168], P(('ctx', 'exp'))
Inputs may be any that keep to these rules, and one draw needn't show every extreme that they name: A permutation: block j of the new tokens (16 rows) sits at positions 512 + block_order[j] * 16 onward. `expert_ids`: each row names 8 different experts; the 4 rows of one device name no expert more than 3 times, and in some aligned block one expert exactly 3 times.
All inputs are finite; a program needn't handle non-finite values.
Results may differ from a plain program's by a relative error of at most 0.012.
Values may be sent and summed in bfloat16 or wider, within the bound.
No kernel may reach another device: no remote copies, remote signals or barrier semaphores. Data moves between devices by JAX's collectives and lax.ppermute only.
A program may use at most 128 MiB of HBM per device.

v0:
```python
import math

import jax
import jax.numpy as jnp
from jax import lax
from jax.sharding import PartitionSpec as P

QKD = 192
CAP = 3


ROUTE_SCALE = 2.5
NORM_EPS = 1e-06


def block_position(row_index, block_order, block_rows):
    blocks = row_index // block_rows
    lookup = blocks[:, None] == jnp.arange(block_order.shape[0], dtype=jnp.int32)[None, :]
    leading = jnp.sum(jnp.where(lookup, block_order[None, :], 0), axis=1)
    return leading * block_rows + row_index % block_rows


def attend(query_lat, query_pe, keys, visible):
    row_count, head_count, latent_width = query_lat.shape
    key_count = keys.shape[1]
    pe_width = query_pe.shape[1] // head_count
    first_dot = jnp.dot(
        query_lat.reshape(row_count * head_count, latent_width),
        keys[:latent_width],
        preferred_element_type=jnp.float32,
    )
    second_dot = jnp.dot(
        query_pe.reshape(row_count * head_count, pe_width),
        keys[latent_width:],
        preferred_element_type=jnp.float32,
    )
    scores = ((first_dot + second_dot) * (1.0 / math.sqrt(QKD))).reshape(
        row_count, head_count, key_count
    )
    scores = jnp.where(visible[:, None, :], scores, -jnp.inf)
    row_max = jnp.max(scores, axis=2)
    exponent = jnp.exp(scores - row_max[:, :, None])
    row_sum = jnp.sum(exponent, axis=2)
    weights = exponent.astype(jnp.bfloat16).reshape(row_count * head_count, key_count)
    latent = lax.dot_general(
        weights, keys[:latent_width], (((1,), (1,)), ((), ())), preferred_element_type=jnp.float32
    )
    return (row_max, row_sum, latent.reshape(row_count, head_count, latent_width))


def merge_partial(earlier, latter):
    highest = latter[0]
    earlier_scale = jnp.exp(earlier[0] - highest)
    latter_scale = jnp.exp(latter[0] - highest)
    row_sum = earlier_scale * earlier[1] + latter_scale * latter[1]
    latent = earlier_scale[:, :, None] * earlier[2] + latter_scale[:, :, None] * latter[2]
    return (highest, row_sum, latent)


def body(
    q_nope,
    q_rope,
    cache_keys,
    fresh_keys,
    block_order,
    w_uv,
    w_out,
    residual,
    norm_gain,
    router_weight,
    expert_ids,
    w_gate,
    w_up,
    w_down,
):
    ctx_count = lax.axis_size("ctx")
    exp_count = lax.axis_size("exp")
    ctx_index = lax.axis_index("ctx")
    rows_here, heads_here, latent_width = q_nope.shape
    value_width = w_uv.shape[2]
    cache_len = cache_keys.shape[1]
    key_cols = cache_len + rows_here
    block_rows = rows_here // 2
    keys_here = jnp.concatenate([cache_keys, fresh_keys], axis=1)
    w_uv_wide = w_uv.astype(jnp.float32)
    own_rows = ctx_index * rows_here + jnp.arange(rows_here, dtype=jnp.int32)
    own_pos = block_position(own_rows, block_order, block_rows)
    start_state = (
        jnp.full((rows_here, heads_here), -jnp.inf, jnp.float32),
        jnp.zeros((rows_here, heads_here), jnp.float32),
        jnp.zeros((rows_here, heads_here, latent_width), jnp.float32),
    )
    portion = lax.all_gather(keys_here, "ctx", axis=1, tiled=True)
    columns = jnp.arange(portion.shape[1], dtype=jnp.int32)
    owner_dev = columns // key_cols
    within = columns % key_cols
    fresh_row = owner_dev * rows_here + within - cache_len
    key_pos = jnp.where(within < cache_len, -1, block_position(fresh_row, block_order, block_rows))
    visible = key_pos[None, :] <= own_pos[:, None]
    row_max, row_sum, latent = merge_partial(start_state, attend(q_nope, q_rope, portion, visible))
    normal_lat = latent / row_sum[:, :, None]
    head_wide = jnp.einsum("rhl,hlv->rhv", normal_lat, w_uv_wide, precision=lax.Precision.HIGHEST)
    head_out = head_wide.astype(jnp.bfloat16).reshape(rows_here, heads_here * value_width)
    tok_here, model_width = residual.shape
    col_part = w_out.shape[1]
    head_partial = jnp.dot(
        lax.all_gather(head_out, "ctx", axis=0, tiled=True),
        w_out,
        preferred_element_type=jnp.float32,
    )
    arranged = head_partial.reshape(ctx_count, exp_count, tok_here, col_part)
    head_total = lax.psum_scatter(
        arranged.astype(jnp.bfloat16), "exp", scatter_dimension=1, tiled=True
    )
    attention = lax.all_to_all(head_total, "ctx", split_axis=0, concat_axis=3, tiled=True).reshape(
        tok_here, model_width
    )
    hidden = residual.astype(jnp.float32) + attention.astype(jnp.float32)
    mean_square = jnp.mean(hidden * hidden, axis=1, keepdims=True)
    normed = (hidden * lax.rsqrt(mean_square + NORM_EPS) * norm_gain).astype(jnp.bfloat16)
    affinity = jax.nn.sigmoid(jnp.dot(normed, router_weight, preferred_element_type=jnp.float32))
    expert_count = router_weight.shape[1]
    onehot = expert_ids[:, :, None] == jnp.arange(expert_count, dtype=jnp.int32)[None, None, :]
    chosen = jnp.sum(jnp.where(onehot, affinity[:, None, :], 0.0), axis=2)
    route = ROUTE_SCALE * chosen / jnp.sum(chosen, axis=1, keepdims=True)
    mixing = jnp.sum(jnp.where(onehot, route[:, :, None], 0.0), axis=1)
    picked = jnp.sum(onehot.astype(jnp.int32), axis=1)
    slot_index = jnp.cumsum(picked, axis=0) - picked
    slot_hot = (slot_index[:, :, None] == jnp.arange(CAP, dtype=jnp.int32)[None, None, :]) & (
        picked[:, :, None] > 0
    )
    dispatch_map = (
        jnp.transpose(slot_hot, (1, 2, 0))
        .reshape(expert_count * CAP, tok_here)
        .astype(jnp.bfloat16)
    )
    send_rows = jnp.dot(dispatch_map, normed, preferred_element_type=jnp.float32).astype(
        jnp.bfloat16
    )
    arrived = lax.all_to_all(
        send_rows.reshape(expert_count, CAP, model_width),
        "exp",
        split_axis=0,
        concat_axis=1,
        tiled=True,
    )
    local_experts = arrived.shape[0]
    portion = lax.all_gather(arrived, "ctx", axis=1, tiled=True)
    gate = jnp.einsum("end,edf->enf", portion, w_gate, preferred_element_type=jnp.float32)
    upward = jnp.einsum("end,edf->enf", portion, w_up, preferred_element_type=jnp.float32)
    activations = (jax.nn.silu(gate) * upward).astype(jnp.bfloat16)
    expert_total = lax.psum_scatter(
        jnp.einsum("enf,efd->ned", activations, w_down, preferred_element_type=jnp.float32).astype(
            jnp.bfloat16
        ),
        "ctx",
        scatter_dimension=0,
        tiled=True,
    )
    going_back = expert_total.reshape(exp_count, CAP, local_experts, model_width)
    returned = lax.all_to_all(going_back, "exp", split_axis=0, concat_axis=2, tiled=True)
    combine_map = jnp.where(slot_hot, mixing[:, :, None], 0.0)
    combine_map = jnp.transpose(combine_map, (0, 2, 1)).reshape(tok_here, CAP * expert_count)
    mixture = jnp.dot(
        combine_map,
        returned.reshape(CAP * expert_count, model_width).astype(jnp.float32),
        precision=lax.Precision.HIGHEST,
    )
    return (hidden + mixture).astype(jnp.bfloat16)


def solution(mesh):
    return jax.shard_map(
        body,
        mesh=mesh,
        in_specs=(
            P("ctx", "exp", None),
            P("ctx", "exp"),
            P(None, "ctx"),
            P(None, "ctx"),
            P(),
            P("exp", None, None),
            P("exp", "ctx"),
            P(("ctx", "exp"), None),
            P(),
            P(),
            P(("ctx", "exp"), None),
            P("exp", None, "ctx"),
            P("exp", None, "ctx"),
            P("exp", "ctx", None),
        ),
        out_specs=P(("ctx", "exp"), None),
        check_vma=False,
    )
```

profile of v0, /device:TPU:0, one launch (start us, length us, event | category | flops | bytes accessed | tf_op | source)
XLA Modules:
  0.0 268.8 jit_solution(8497776579315052715)
XLA Ops:
  8.2 1.0 reshape.299
  9.2 1.1 copy.39
  11.1 10.3 %all_gather.9 = bf16[576,640]{0,1:T(8,128)(2,1)S(1)} all-gather(bf16[576,160]{0,1:T(8,128)(2,1)S(1)} %pad_maximum_fusion), channel_id=1, replica_groups=mesh['ctx'=4,'exp'=8] {'ctx'}, dimensions={1}, use_global_device_ids=true | all-gather | bytes 921600 | tf_op jit(solution)/shard_map/all_gather | solution.py:93
  21.4 1.6 fusion.16
  23.7 1.1 fusion.8
  25.3 1.7 fusion.6
  27.0 1.0 fusion.10
  28.1 7.3 %all_gather.10 = bf16[128,2048]{1,0:T(8,128)(2,1)S(1)} all-gather(bf16[32,2048]{1,0:T(8,128)(2,1)S(1)} %bitcast.75), channel_id=1, replica_groups=mesh['ctx'=4,'exp'=8] {'ctx'}, dimensions={0}, use_global_device_ids=true | all-gather | bytes 655360 | tf_op jit(solution)/shard_map/all_gather | solution.py:107
  35.3 4.2 %convolution_convert_fusion.2 = bf16[128,1792]{1,0:T(8,128)(2,1)S(1)} fusion(bf16[128,2048]{1,0:T(8,128)(2,1)S(1)} %all_gather.10, bf16[2048,1792]{1,0:T(8,128)(2,1)} %param.20), kind=kOutput, calls=%fused_computation.5 | convolution fusion | flops 939753472 | bytes 8323072 | tf_op jit(solution)/shard_map/dot_general | solution.py:106
  41.2 72.6 %all-reduce.3.cloned.1.call-done = bf16[4,8,4,1792]{3,2,1,0:T(4,128)(2,1)} async-done(((bf16[4,8,4,1792]{3,2,1,0:T(4,128)(2,1)}), bf16[4,8,4,1792]{3,2,1,0:T(4,128)(2,1)}) %all-reduce.3.cloned.1.call-update) | async-done | bytes 458768
  113.9 2.1 constant_dynamic-slice_fusion
  115.9 3.3 %all-to-all-start = ((bf16[4,1,4,1792]{3,2,1,0:T(4,128)(2,1)}), bf16[4,1,4,1792]{3,2,1,0:T(4,128)(2,1)S(1)}, u32[]{:S(2)}, u32[]{:S(2)}) async-start(bf16[4,1,4,1792]{3,2,1,0:T(4,128)(2,1)} %constant_dynamic-slice_fusion), calls=%async_computation | async-start | bytes 114688 | tf_op jit(solution)/shard_map/all_to_all | solution.py:115
  119.8 3.5 %all-to-all-done = bf16[4,1,4,1792]{3,2,1,0:T(4,128)(2,1)S(1)} async-done(((bf16[4,1,4,1792]{3,2,1,0:T(4,128)(2,1)}), bf16[4,1,4,1792]{3,2,1,0:T(4,128)(2,1)S(1)}, u32[]{:S(2)}, u32[]{:S(2)}) %all-to-all-start) | async-done | bytes 57376 | tf_op jit(solution)/shard_map/all_to_all | solution.py:115
  124.8 26.9 %all_to_all.42 = bf16[16,3,7168]{2,1,0:T(4,128)(2,1)S(1)} all-to-all(bf16[16,3,7168]{2,1,0:T(4,128)(2,1)S(1)} %reshape.301), channel_id=1, replica_groups=mesh['ctx'=4,'exp'=8] {'exp'}, dimensions={0} | all-to-all | bytes 1376256 | tf_op jit(solution)/shard_map/all_to_all | solution.py:140
  153.5 23.9 %all-gather.2.cloned.1.call-done = bf16[2,96,7168]{2,1,0:T(8,128)(2,1)} async-done(((bf16[2,24,7168]{2,1,0:T(8,128)(2,1)}), bf16[2,96,7168]{2,1,0:T(8,128)(2,1)}) %all-gather.2.cloned.1.call-update) | async-done | bytes 2752528 | tf_op jit(solution)/shard_map/all_gather | solution.py:148
  177.4 8.6 %fusion.40 = f32[2,96,512]{2,1,0:T(8,128)S(1)} fusion(bf16[2,96,7168]{2,1,0:T(8,128)(2,1)} %all-gather.2.cloned.1.call-done, bf16[2,7168,512]{2,1,0:T(8,128)(2,1)} %param.25), kind=kOutput, calls=%fused_computation.91 | convolution fusion | flops 1409286144 | bytes 17825792 | tf_op jit(solution)/shard_map/end,edf->enf/dot_general | solution.py:149
  186.0 7.8 %fusion.7 = bf16[2,96,512]{2,1,0:T(8,128)(2,1)S(1)} fusion(bf16[2,96,7168]{2,1,0:T(8,128)(2,1)S(1)} %copy-done.2, bf16[2,7168,512]{2,1,0:T(8,128)(2,1)} %param.26, f32[2,96,512]{2,1,0:T(8,128)S(1)} %fusion.40), kind=kOutput, calls=%fused_computation.15 | convolution fusion | flops 1409875968 | bytes 18022400 | tf_op jit(solution)/shard_map/end,edf->enf/dot_general | solution.py:150
  193.8 2.6 fusion
  196.4 1.8 copy.56
  198.2 35.5 %reduce-scatter.5.cloned.1.call-done = bf16[24,14336]{1,0:T(8,128)(2,1)} async-done(((bf16[96,14336]{1,0:T(8,128)(2,1)}), bf16[24,14336]{1,0:T(8,128)(2,1)}) %reduce-scatter.5.cloned.1.call-update) | async-done | bytes 688144
  233.7 2.6 reshape.310
  236.3 5.5 %all-to-all-start.2 = ((bf16[8,3,2,7168]{3,2,1,0:T(2,128)(2,1)}), bf16[8,3,2,7168]{3,2,1,0:T(2,128)(2,1)S(1)}, u32[]{:S(2)}, u32[]{:S(2)}) async-start(bf16[8,3,2,7168]{3,2,1,0:T(2,128)(2,1)} %bitcast.15), calls=%async_computation.2 | async-start | bytes 1376256 | tf_op jit(solution)/shard_map/all_to_all | solution.py:161
  242.5 17.2 %all-to-all-done.2 = bf16[8,3,2,7168]{3,2,1,0:T(2,128)(2,1)S(1)} async-done(((bf16[8,3,2,7168]{3,2,1,0:T(2,128)(2,1)}), bf16[8,3,2,7168]{3,2,1,0:T(2,128)(2,1)S(1)}, u32[]{:S(2)}, u32[]{:S(2)}) %all-to-all-start.2) | async-done | bytes 688160 | tf_op jit(solution)/shard_map/all_to_all | solution.py:161
  260.4 1.9 fusion.1
  (81 shorter events, 10.5 us)
Async XLA Ops:
  6.5 20.5 %copy-start = (bf16[16,512,128]{2,1,0:T(8,128)(2,1)S(1)}, bf16[16,512,128]{2,1,0:T(8,128)(2,1)}, u32[]{:S(2)}) copy-start(bf16[16,512,128]{2,1,0:T(8,128)(2,1)} %param.19) | copy-start | bytes 6291460
  6.5 107.3 %all-reduce.3.cloned.1.call-start = ((), (), s32[]{:S(2)}) async-start(), calls=%async_computation.6 | async-start | bytes 917504
  35.3 5.2 %copy-start.8 = (u32[32]{0:T(128)S(1)}, u32[32]{0:T(128)}, u32[]{:S(2)}) copy-start(u32[32]{0:T(128)} %constant.104) | copy-start | bytes 388
  35.3 5.8 %copy-start.6 = (s32[4,8]{1,0:T(4,128)S(1)}, s32[4,8]{1,0:T(4,128)}, u32[]{:S(2)}) copy-start(s32[4,8]{1,0:T(4,128)} %param.24) | copy-start | bytes 388
  35.3 87.9 %copy-start.4 = (bf16[4,7168]{1,0:T(4,128)(2,1)S(1)}, bf16[4,7168]{1,0:T(4,128)(2,1)}, u32[]{:S(2)}) copy-start(bf16[4,7168]{1,0:T(4,128)(2,1)} %param.21) | copy-start | bytes 172036
  35.3 88.1 %copy-start.5 = (f32[7168]{0:T(1024)S(1)}, f32[7168]{0:T(1024)}, u32[]{:S(2)}) copy-start(f32[7168]{0:T(1024)} %param.22) | copy-start | bytes 86020
  115.9 7.3 %all-to-all-start = ((bf16[4,1,4,1792]{3,2,1,0:T(4,128)(2,1)}), bf16[4,1,4,1792]{3,2,1,0:T(4,128)(2,1)S(1)}, u32[]{:S(2)}, u32[]{:S(2)}) async-start(bf16[4,1,4,1792]{3,2,1,0:T(4,128)(2,1)} %constant_dynamic-slice_fusion), calls=%async_computation | async-start | bytes 114688 | tf_op jit(solution)/shard_map/all_to_all | solution.py:115
  119.2 58.2 %all-gather.2.cloned.1.call-start = ((), (), s32[]{:S(2)}) async-start(), calls=%async_computation.4 | async-start | bytes 3440640 | tf_op jit(solution)/shard_map/all_gather | solution.py:148
  123.3 0.7 copy-start.3
  153.2 80.5 %reduce-scatter.5.cloned.1.call-start = ((), (), s32[]{:S(2)}) async-start(), calls=%async_computation.5 | async-start | bytes 3440640
  177.4 8.6 %copy-start.2 = (bf16[2,96,7168]{2,1,0:T(8,128)(2,1)S(1)}, bf16[2,96,7168]{2,1,0:T(8,128)(2,1)}, u32[]{:S(2)}) copy-start(bf16[2,96,7168]{2,1,0:T(8,128)(2,1)} %all-gather.2.cloned.1.call-done) | copy-start | bytes 8257540
  177.4 16.4 %slice-start = ((s8[14680064]{0:T(1024)(128)(4,1)}), s8[4194304]{0:T(1024)(128)(4,1)S(1)}, s32[]{:S(2)}) async-start(s8[14680064]{0:T(1024)(128)(4,1)} %bitcast.63), calls=%async_computation.7 | async-start | bytes 8388608
  177.4 16.4 %slice-start.1 = ((s8[14680064]{0:T(1024)(128)(4,1)}), s8[4194304]{0:T(1024)(128)(4,1)S(1)}, s32[]{:S(2)}) async-start(s8[14680064]{0:T(1024)(128)(4,1)} %bitcast.63), calls=%async_computation.8 | async-start | bytes 8388608
  186.0 7.8 %slice-start.2 = ((s8[14680064]{0:T(1024)(128)(4,1)}), s8[4194304]{0:T(1024)(128)(4,1)S(1)}, s32[]{:S(2)}) async-start(s8[14680064]{0:T(1024)(128)(4,1)} %bitcast.63), calls=%async_computation.9 | async-start | bytes 8388608
  186.0 7.8 %slice-start.3 = ((s8[14680064]{0:T(1024)(128)(4,1)}), s8[2097152]{0:T(1024)(128)(4,1)S(1)}, s32[]{:S(2)}) async-start(s8[14680064]{0:T(1024)(128)(4,1)} %bitcast.63), calls=%async_computation.10 | async-start | bytes 4194304
  198.2 43.6 %copy-start.7 = (bf16[7168,16]{0,1:T(8,128)(2,1)S(1)}, bf16[7168,16]{0,1:T(8,128)(2,1)}, u32[]{:S(2)}) copy-start(bf16[7168,16]{0,1:T(8,128)(2,1)} %param.23) | copy-start | bytes 688132
  233.7 28.6 %copy-start.1 = (bf16[16,512,128]{2,1,0:T(8,128)(2,1)S(1)}, bf16[16,512,128]{2,1,0:T(8,128)(2,1)}, u32[]{:S(2)}) copy-start(bf16[16,512,128]{2,1,0:T(8,128)(2,1)} %param.19) | copy-start | bytes 6291460
  236.3 23.4 %all-to-all-start.2 = ((bf16[8,3,2,7168]{3,2,1,0:T(2,128)(2,1)}), bf16[8,3,2,7168]{3,2,1,0:T(2,128)(2,1)S(1)}, u32[]{:S(2)}, u32[]{:S(2)}) async-start(bf16[8,3,2,7168]{3,2,1,0:T(2,128)(2,1)} %bitcast.15), calls=%async_computation.2 | async-start | bytes 1376256 | tf_op jit(solution)/shard_map/all_to_all | solution.py:161
Sparse Core Ops, SparseCore 0:
  40.6 73.1 all-reduce.2
  153.3 23.9 all-gather.1
  198.3 35.3 reduce-scatter.4
where the time goes:
time: 270 us; the launch traced here: 269 us
  waiting for transfers between devices  153 us (57%)
  blocking collectives  44.4 us (16%)
  matrix products  30.6 us (11%)
  local copies, waits for them, and re-layouts  14.2 us (5%)
  between operations  13.4 us (5%)
  starting transfers between devices  9.06 us (3%)
  other arithmetic  4.49 us (2%)
    unnamed x5, waiting for transfers between devices  108 us
    all_to_all x1, blocking collectives, body(): lax.all_to_all(send_rows.reshape(expert_count, CAP, model_width), 'exp',...  26.9 us
    all_gather x1, waiting for transfers between devices, body(): portion = lax.all_gather(arrived, 'ctx', axis=1, tiled=True)  23.9 us
    all_to_all x1, waiting for transfers between devices, body(): lax.all_to_all(going_back, 'exp', split_axis=0, concat_axis=2, tiled=True)  17.2 us
    all_gather x1, blocking collectives, body(): portion = lax.all_gather(keys_here, 'ctx', axis=1, tiled=True)  10.3 us
    dot_general x1, matrix products, body(): jnp.einsum('end,edf->enf', portion, w_gate, preferred_element_type=jnp.fl...  8.57 us
    dot_general x1, matrix products, body(): jnp.einsum('end,edf->enf', portion, w_up, preferred_element_type=jnp.floa...  7.8 us
    all_gather x1, blocking collectives, body(): lax.all_gather(head_out, 'ctx', axis=0, tiled=True)  7.27 us
  transfers between devices with their start and end apart: 5, of which 5 were waited for; matrix products, arithmetic and copies ran while one was open for 1% of the time, Pallas kernels for 0%

commit v1 on v0

v1 whole, which is shorter than its diff:
```python
import math

import jax
import jax.numpy as jnp
from jax import lax
from jax.experimental import pallas as pl
from jax.experimental.pallas import tpu as pltpu
from jax.sharding import PartitionSpec as P


QKD = 192
ROUTE_SCALE = 2.5
NORM_EPS = 1e-06
EXTRA = 128
IDS = 16
BF = jnp.bfloat16
F32 = jnp.float32
I32 = jnp.int32
NT = (((1,), (1,)), ((), ()))


def bits_of(count):
    masks = []
    bit = 1
    while bit < count:
        masks.append(bit)
        bit *= 2
    return masks


def subsets(masks):
    out = [0]
    for m in masks:
        out = out + [s | m for s in out]
    return out


def held(x):
    return pltpu.with_memory_space_constraint(x, pltpu.VMEM)


def dot(a, b):
    return jnp.dot(a, b, preferred_element_type=F32)


def dot_t(a, b):
    return lax.dot_general(a, b, NT, preferred_element_type=F32)


def call(kernel, outs, args, specs, limit, flops, loads=(), scratch=()):
    shapes = [jax.ShapeDtypeStruct(s, d) for s, d in outs]
    shapes += [pltpu.VMEM(s, BF) for s in loads]
    args = [
        pltpu.with_memory_space_constraint(a, pltpu.HBM) if s == pltpu.HBM else a
        for a, s in zip(args, specs)
    ]
    got = pl.pallas_call(
        kernel,
        out_shape=tuple(shapes),
        in_specs=[pl.BlockSpec(memory_space=s) for s in specs],
        out_specs=tuple(pl.BlockSpec(memory_space=pltpu.VMEM) for _ in shapes),
        scratch_shapes=list(scratch),
        compiler_params=pltpu.CompilerParams(vmem_limit_bytes=limit << 20),
        cost_estimate=pl.CostEstimate(flops=flops, bytes_accessed=0, transcendentals=0),
    )(*args)
    return list(got)


def pick(index, table):
    out = jnp.zeros(index.shape, I32)
    for i, v in enumerate(table):
        out = jnp.where(index == i, v, out)
    return out


def attend(meta, q, qr, kc, kf, w_uv, w_out, korder, block_rows):
    nctx = len(kc)
    kd, cache_len = kc[0].shape
    rows = kf[0].shape[0]
    heads, lat, vh = w_uv.shape
    group = max(1, 128 // rows)
    nblk = meta.shape[0] - 2

    def kernel(*refs):
        idx_ref, q_ref, qr_ref = refs[:3]
        kc_ref = refs[3 : 3 + nctx]
        kf_ref = refs[3 + nctx : 3 + 2 * nctx]
        w_hbm, wo_hbm, out_ref, wo_ref, w_ref, sems = refs[3 + 2 * nctx :]
        load = pltpu.make_async_copy(w_hbm, w_ref, sems.at[0])
        load.start()
        load_out = pltpu.make_async_copy(wo_hbm, wo_ref, sems.at[1])
        load_out.start()
        c = idx_ref[0]
        starts = [idx_ref[2 + b] * block_rows for b in range(nblk)]

        def position(grow):
            return pick(grow // block_rows, starts) + grow % block_rows

        kfa = jnp.concatenate([k[...] for k in kf_ref], axis=0)
        kca = jnp.concatenate([k[...] for k in kc_ref], axis=1)
        col = lax.broadcasted_iota(I32, (1, nctx * rows), 1)
        owner = pick(col // rows, [c ^ k for k in korder])
        kpos = position(owner * rows + col % rows)
        row = lax.broadcasted_iota(I32, (group * rows, 1), 0)
        qpos = position(c * rows + row % rows)
        visible = kpos <= qpos
        scale = 1.0 / math.sqrt(QKD)
        for g in range(heads // group):
            lo = g * group * rows
            qb = q_ref[lo : lo + group * rows, :]
            rb = qr_ref[lo : lo + group * rows, :]
            sc = (dot(qb, kca[:lat]) + dot(rb, kca[lat:])) * scale
            sf = (dot_t(qb, kfa[:, :lat]) + dot_t(rb, kfa[:, lat:])) * scale
            sf = jnp.where(visible, sf, -jnp.inf)
            top = jnp.maximum(
                jnp.max(sc, axis=1, keepdims=True), jnp.max(sf, axis=1, keepdims=True)
            )
            pc = jnp.exp(sc - top)
            pf = jnp.exp(sf - top)
            total = jnp.sum(pc, axis=1, keepdims=True) + jnp.sum(pf, axis=1, keepdims=True)
            acc = dot_t(pc.astype(BF), kca[:lat]) + dot(pf.astype(BF), kfa[:, :lat])
            acc = acc / total
            hi = acc.astype(BF)
            low = (acc - hi.astype(F32)).astype(BF)
            if g == 0:
                load.wait()
            for h in range(group):
                w = w_ref[g * group + h]
                a = h * rows
                v = dot(hi[a : a + rows], w) + dot(low[a : a + rows], w)
                n = (g * group + h) * vh
                out_ref[:, n : n + vh] = v.astype(BF)
        load_out.wait()

    specs = (pltpu.SMEM,) + (pltpu.VMEM,) * (2 + 2 * nctx) + (pltpu.HBM,) * 2
    flops = 2 * heads * rows * nctx * (cache_len + rows) * (kd + lat)
    return call(
        kernel,
        [((rows, heads * vh), BF)],
        (meta, q, qr, *kc, *kf, w_uv, w_out),
        specs,
        16,
        flops,
        [w_out.shape],
        [pltpu.VMEM(w_uv.shape, BF), pltpu.SemaphoreType.DMA((2,))],
    )


def project(idx, hg, w_out, korder, emasks, tok):
    nctx = len(hg)
    rows, width = hg[0].shape
    total = nctx * rows
    cols = w_out.shape[1]

    def kernel(idx_ref, *refs):
        hg_ref = refs[:nctx]
        w_ref, send_ref, keep_ref = refs[nctx:]
        c = idx_ref[0]
        e = idx_ref[1]
        r = lax.broadcasted_iota(I32, (total, 1), 0)
        place = [0] * nctx
        for i, k in enumerate(korder):
            place[k] = i
        kp = jnp.zeros(r.shape, I32)
        rel = (r // tok) % nctx
        for k in range(nctx):
            kp = jnp.where(rel == (c ^ k), place[k], kp)
        j = pick(r // (nctx * tok), [e ^ m for m in emasks])
        src = kp * rows + j * tok + r % tok
        perm = (src == lax.broadcasted_iota(I32, (total, total), 1)).astype(F32).astype(BF)
        lhs = dot(perm, jnp.concatenate([h[...] for h in hg_ref], axis=0)).astype(BF)
        half = total // 2
        full = dot(lhs, w_ref[...])
        send_ref[...] = full[half:].astype(BF)
        keep_ref[...] = full[:half]

    return call(
        kernel,
        [((total // 2, cols), BF), ((total // 2, cols), F32)],
        (idx, *hg, held(w_out)),
        (pltpu.SMEM,) + (pltpu.VMEM,) * (nctx + 1),
        12,
        2 * total * width * cols,
    )


def choose(pairs):
    out = None
    for cond, x in pairs:
        x = jnp.where(cond, x, 0.0)
        out = x if out is None else out + x
    return out


def residual_parts(idx, residual, ids, nctx):
    tok, width = residual.shape
    cols = width // nctx
    top = ids.shape[1]

    def kernel(idx_ref, res_ref, ids_ref, *outs):
        c = idx_ref[0]
        lane = lax.broadcasted_iota(I32, (tok, EXTRA), 1)
        side = jnp.zeros((tok, EXTRA), F32)
        for t in range(top):
            side = jnp.where(lane - IDS == ids_ref[:, t : t + 1], 1.0, side)
        res = res_ref[...].astype(F32)
        for k in range(nctx):
            outs[k][:, :cols] = choose(
                [((c ^ k) == j, res[:, j * cols : (j + 1) * cols]) for j in range(nctx)]
            ).astype(BF)
            outs[k][:, cols:] = side.astype(BF)

    return call(
        kernel,
        [((tok, cols + EXTRA), BF)] * nctx,
        (idx, residual, ids),
        (pltpu.SMEM, pltpu.VMEM, pltpu.VMEM),
        4,
        1 << 28,
    )


def one_hot_rows(out_rows, in_rows, tok, shift):
    r = lax.broadcasted_iota(I32, (out_rows, in_rows), 0)
    q = lax.broadcasted_iota(I32, (out_rows, in_rows), 1)
    return ((r == q + shift * tok)).astype(F32).astype(BF)


def merge(idx, parts, own, got, gain, tok):
    nctx = len(parts)
    blk, cols = own.shape
    hc = cols // 2
    n = len(got)

    def kernel(idx_ref, *refs):
        c = idx_ref[0]
        prefs = refs[:nctx]
        own_ref = refs[nctx]
        grefs = refs[nctx + 1 : nctx + 1 + n]
        gain_ref, sx_ref, att_ref = refs[nctx + 1 + n :]
        att = own_ref[...]
        for g in grefs:
            att = att + g[...].astype(F32)
        att = att.astype(BF)
        att_ref[...] = att
        res = None
        for k in range(nctx):
            part = dot(one_hot_rows(blk, tok, tok, c ^ k), prefs[k][...])
            res = part if res is None else res + part
        hidden = res[:, :cols] + att.astype(F32)
        ssq = jnp.sum(hidden * hidden, axis=1, keepdims=True)
        gain = choose(
            [(c == j, gain_ref[:, j * cols : (j + 1) * cols]) for j in range(nctx)]
        )
        scaled = hidden * gain
        hi = ssq.astype(BF).astype(F32)
        mid = (ssq - hi).astype(BF).astype(F32)
        low = ssq - hi - mid
        extra = res[:, cols:]
        lane = lax.broadcasted_iota(I32, extra.shape, 1)
        extra = jnp.where(lane == 0, hi, jnp.where(lane == 1, mid, extra))
        extra = jnp.where(lane == 2, low, extra)
        sx_ref[:, :hc] = scaled[:, :hc].astype(BF)
        sx_ref[:, hc : hc + EXTRA] = extra.astype(BF)
        sx_ref[:, hc + EXTRA :] = scaled[:, hc:].astype(BF)

    return call(
        kernel,
        [((blk, cols + EXTRA), BF), ((blk, cols), BF)],
        (idx, *parts, own, *got, gain),
        (pltpu.SMEM,) + (pltpu.VMEM,) * (nctx + n + 2),
        4,
        1 << 28,
    )


def attention_parts(idx, att, nctx, tok):
    cols = att.shape[1]

    def kernel(idx_ref, att_ref, *outs):
        c = idx_ref[0]
        r = lax.broadcasted_iota(I32, (tok, nctx * tok), 0)
        q = lax.broadcasted_iota(I32, (tok, nctx * tok), 1)
        for k in range(nctx):
            pickr = (q == r + (c ^ k) * tok).astype(F32).astype(BF)
            outs[k][...] = dot(pickr, att_ref[...]).astype(BF)

    return call(
        kernel,
        [((tok, cols), BF)] * nctx,
        (idx, att),
        (pltpu.SMEM, pltpu.VMEM),
        4,
        1 << 28,
    )


def finalize(idx, residual, parts, own, got):
    nctx = len(parts)
    tok, width = residual.shape
    cols = width // nctx
    n = len(got)

    def kernel(idx_ref, res_ref, *refs):
        c = idx_ref[0]
        prefs = [p[...].astype(F32) for p in refs[:nctx]]
        own_ref = refs[nctx]
        grefs = refs[nctx + 1 : nctx + 1 + n]
        out_ref = refs[nctx + 1 + n]
        for j in range(nctx):
            a, b = j * cols, (j + 1) * cols
            att = choose([((c ^ k) == j, prefs[k]) for k in range(nctx)])
            mix = own_ref[:, a:b]
            for g in grefs:
                mix = mix + g[:, a:b].astype(F32)
            out_ref[:, a:b] = (res_ref[:, a:b].astype(F32) + att + mix).astype(BF)

    return call(
        kernel,
        [((tok, width), BF)],
        (idx, residual, *parts, own, *got),
        (pltpu.SMEM,) + (pltpu.VMEM,) * (nctx + n + 2),
        4,
        1 << 28,
    )[0]


class Chunk:
    def __init__(self, pieces, mask, half):
        self.pieces = pieces
        self.mask = mask
        self.half = half


def grab(arrays):
    n = len(arrays)

    def kernel(*refs):
        tok_ref = refs[n]
        sems = refs[2 * n + 1]
        copies = []
        for i in range(n):
            copies.append(pltpu.make_async_copy(refs[i], refs[n + 1 + i], sems.at[i]))
            copies[-1].start()
        tok_ref[...] = jnp.zeros(tok_ref.shape, F32)
        for cp in copies:
            cp.wait()

    done, *got = call(
        kernel,
        [((8, 128), F32)],
        tuple(arrays),
        (pltpu.HBM,) * n,
        1,
        1 << 30,
        [a.shape for a in arrays],
        [pltpu.SemaphoreType.DMA((n,))],
    )
    return done, got


def fetch(idx, blocks, w_gate, w_up, hc):
    local, _, ff = w_gate.shape
    n = len(blocks)

    def kernel(idx_ref, wg_ref, wu_ref, tok_ref, *refs):
        sems = refs[2 * n]
        copies = []
        for i, (mask, half) in enumerate(blocks):
            start = pl.multiple_of(((idx_ref[0] ^ mask) * 2 + half) * hc, 16)
            for j, src in enumerate((wg_ref, wu_ref)):
                cp = pltpu.make_async_copy(
                    src.at[:, pl.ds(start, hc), :], refs[2 * i + j], sems.at[i, j]
                )
                cp.start()
                copies.append(cp)
        tok_ref[...] = jnp.zeros(tok_ref.shape, F32)
        for cp in copies:
            cp.wait()

    shape = (local, hc, ff)
    done, *got = call(
        kernel,
        [((8, 128), F32)],
        (idx, w_gate, w_up),
        (pltpu.SMEM, pltpu.HBM, pltpu.HBM),
        1,
        1 << 30,
        [shape] * (2 * n),
        [pltpu.SemaphoreType.DMA((n, 2))],
    )
    return done, {b: (got[2 * i], got[2 * i + 1]) for i, b in enumerate(blocks)}


def experts(idx, chunks, router, weights, width, carry, finish):
    loaded = [held(w) for ch in chunks for w in weights[ch.mask, ch.half]]
    local, hc, ff = loaded[0].shape
    nw = len(loaded)
    pieces = [p for ch in chunks for p in ch.pieces]
    total = sum(p.shape[0] for p in chunks[0].pieces)
    nexperts = router.shape[1]
    n = len(pieces)
    ncarry = len(carry)

    def kernel(*refs):
        idx_ref = refs[0]
        prefs = refs[1 : 1 + n]
        r_ref = refs[1 + n]
        wrefs = refs[2 + n : 2 + n + nw]
        crefs = refs[2 + n + nw : 2 + n + nw + ncarry]
        outs = refs[2 + n + nw + ncarry :]
        c = idx_ref[0]
        xs = []
        at = 0
        logit = crefs[2][...] if ncarry else jnp.zeros((total, nexperts), F32)
        ssum = crefs[3][...] if ncarry else jnp.zeros((total, 1), F32)
        for ch in chunks:
            parts = [prefs[at + i][...] for i in range(len(ch.pieces))]
            at += len(parts)
            x = parts[0] if len(parts) == 1 else jnp.concatenate(parts, axis=0)
            block = (c ^ ch.mask) * 2 + ch.half
            if ch.half == 0:
                extra = x[:, hc : hc + EXTRA].astype(F32)
                lane = lax.broadcasted_iota(I32, extra.shape, 1)
                ssum = ssum + jnp.sum(jnp.where(lane < 3, extra, 0.0), axis=1, keepdims=True)
                chosen = extra[:, IDS : IDS + nexperts]
            x = x[:, :hc]
            xs.append(x)
            logit = logit + dot_t(x, r_ref[block])
        if finish is None:
            for e in range(local):
                for c_i in (0, 1):
                    acc = crefs[c_i][e] if ncarry else None
                    for i, x in enumerate(xs):
                        part = dot(x, wrefs[2 * i + c_i][e])
                        acc = part if acc is None else acc + part
                    outs[c_i][e] = acc
            outs[2][...] = logit
            outs[3][...] = ssum
            return
        scale = lax.rsqrt(ssum / width + NORM_EPS)
        affinity = jax.nn.sigmoid(logit * scale) * chosen
        mixing = ROUTE_SCALE * affinity / jnp.sum(affinity, axis=1, keepdims=True)
        lane = lax.broadcasted_iota(I32, mixing.shape, 1)
        acts = []
        for e in range(local):
            vals = []
            for c_i in (0, 1):
                acc = crefs[c_i][e]
                for i, x in enumerate(xs):
                    acc = acc + dot(x, wrefs[2 * i + c_i][e])
                vals.append(acc * scale)
            mine = idx_ref[1] * local + e
            mix = jnp.sum(jnp.where(lane == mine, mixing, 0.0), axis=1, keepdims=True)
            acts.append((jax.nn.silu(vals[0]) * vals[1] * mix).astype(BF))
        act = jnp.concatenate(acts, axis=1)
        nctx, tok, order_in, plans = finish
        r = lax.broadcasted_iota(I32, (total, 1), 0)
        for plan, out_ref in zip(plans, outs):
            pos = r // tok
            cm = pick(pos, [a for a, _ in plan])
            where_in = [order_in.index(b) for _, b in plan]
            p = pick(pos, where_in)
            src = (p * nctx + (c ^ cm)) * tok + r % tok
            perm = (src == lax.broadcasted_iota(I32, (total, total), 1)).astype(F32).astype(BF)
            out_ref[...] = dot(perm, act).astype(BF)

    acc_shape = (local, total, ff)
    if finish is None:
        outs = [(acc_shape, F32), (acc_shape, F32), ((total, nexperts), F32), ((total, 1), F32)]
    else:
        outs = [((total, local * ff), BF), ((total, local * ff), BF)]
    args = (idx, *pieces, router, *loaded, *carry)
    specs = (pltpu.SMEM,) + (pltpu.VMEM,) * (len(args) - 1)
    flops = len(chunks) * 4 * total * hc * ff * local
    return call(kernel, outs, args, specs, 8, flops)


def down(lhs, w_down, lo):
    total = lhs.shape[0]
    local, ff, width = w_down.shape
    hw = width // 2

    def kernel(x_ref, w_ref, send_ref, keep_ref):
        half = total // 2
        step = hw // 4
        for i in range(4):
            acc = None
            for e in range(local):
                part = dot(
                    x_ref[:, e * ff : (e + 1) * ff],
                    w_ref[e, :, lo + i * step : lo + (i + 1) * step],
                )
                acc = part if acc is None else acc + part
            send_ref[:, i * step : (i + 1) * step] = acc[half:].astype(BF)
            keep_ref[:, i * step : (i + 1) * step] = acc[:half]

    return call(
        kernel,
        [((total // 2, hw), BF), ((total // 2, hw), F32)],
        (lhs, held(w_down)),
        (pltpu.VMEM, pltpu.VMEM),
        8,
        2 * total * local * ff * hw,
    )


def body(
    q_nope,
    q_rope,
    cache_keys,
    fresh_keys,
    block_order,
    w_uv,
    w_out,
    residual,
    norm_gain,
    router_weight,
    expert_ids,
    w_gate,
    w_up,
    w_down,
):
    nctx = lax.axis_size("ctx")
    nexp = lax.axis_size("exp")
    c = lax.axis_index("ctx")
    e = lax.axis_index("exp")
    idx = jnp.stack([c, e]).astype(I32)
    cmasks = bits_of(nctx)
    emasks = bits_of(nexp)
    core, xs = cmasks[0], cmasks[1:]
    ym, zs = emasks[0], emasks[1:]
    zsub = subsets(zs)
    eorder = [y ^ z for y in (0, ym) for z in zsub]

    def swap(x, cm=0, em=0):
        m = cm * nexp + em
        return lax.ppermute(x, ("ctx", "exp"), [(i, i ^ m) for i in range(nctx * nexp)])

    rows_here, heads_here, lat = q_nope.shape
    tok, width = residual.shape
    cols = w_out.shape[1]
    hc = cols // 2
    total_rows = nctx * rows_here
    nexperts = router_weight.shape[1]
    block_rows = total_rows // block_order.shape[0]
    pe = q_rope.shape[1] // heads_here

    def spread(group):
        sets = [[x] for x in group]
        for m in xs:
            sets = [got + [swap(g, cm=m) for g in got] for got in sets]
        return [got + [swap(g, cm=core) for g in got] for got in sets]

    korder = subsets(xs)
    korder = korder + [k ^ core for k in korder]

    kf_own = fresh_keys.T
    kc_v, kf_v = grab((cache_keys, kf_own))[1]
    q = q_nope.transpose(1, 0, 2).reshape(heads_here * rows_here, lat)
    qr = q_rope.reshape(rows_here, heads_here, pe).transpose(1, 0, 2)
    qr = qr.reshape(heads_here * rows_here, pe)
    meta = jnp.concatenate([idx, block_order])
    kc, kf = spread((cache_keys, kf_own))
    kc[0], kf[0] = held(kc_v), held(kf_v)
    head, w_out_v = attend(meta, q, qr, kc, kf, w_uv, w_out, korder, block_rows)

    xorder = subsets(xs)
    nx = len(xorder)
    order = [(m, h) for m in xorder for h in (0, 1)]
    order = order + [(m ^ core, h) for m, h in order]
    count = len(order)
    weights = {}
    for lo, hi in FETCHES:
        part = order[count * lo // 8 : count * hi // 8]
        weights.update(fetch(idx, part, w_gate, w_up, hc)[1])
    down_v = grab((w_down,))[1][0]

    res_got = residual_parts(idx, residual, expert_ids, nctx)
    res_got = [swap(p, cm=k) if k else p for k, p in enumerate(res_got)]

    (hg,) = spread((head,))
    send, keep = project(idx, hg, w_out_v, korder, eorder, tok)

    summed = keep + swap(send, em=ym).astype(F32)
    blk = nctx * tok
    got = [
        swap(summed[i * blk : (i + 1) * blk].astype(BF), em=m)
        for i, m in enumerate(zsub)
        if m
    ]
    sx, att_blk = merge(idx, res_got, summed[:blk], got, norm_gain[None], tok)

    zx = jnp.stack([swap(sx, em=m) if m else sx for m in zsub])
    zx = zx.reshape(len(zsub) * blk, -1)
    za = zx[:, : hc + EXTRA][None]
    zb = zx[:, hc + EXTRA :][None]
    own_a = jnp.concatenate([za, swap(za, em=ym)], axis=1)
    xb = zb
    for m in xs:
        xb = jnp.concatenate([xb, swap(xb, cm=m)], axis=0)
    far_b = swap(xb, em=ym)
    xa = own_a
    for m in xs:
        xa = jnp.concatenate([xa, swap(xa, cm=m)], axis=0)
    own_a_core = swap(own_a, cm=core)
    xb_core = swap(xb, cm=core)
    rest_a = xa[1:]
    rest_a_core = swap(rest_a, cm=core)
    far_b_core = swap(far_b, cm=core)

    router = router_weight.reshape(2 * nctx, hc, nexperts).transpose(0, 2, 1)
    first = [Chunk([own_a[0]], 0, 0)]
    g1 = experts(idx, first, router, weights, width, (), None)
    second = [Chunk([rest_a[i - 1]], xorder[i], 0) for i in range(1, nx)]
    second += [Chunk([xb[i], far_b[i]], xorder[i], 1) for i in range(nx)]
    g2 = experts(idx, second, router, weights, width, g1, None)
    third = [Chunk([own_a_core[0]], core, 0)]
    third += [Chunk([rest_a_core[i - 1]], core ^ xorder[i], 0) for i in range(1, nx)]
    third += [Chunk([xb_core[i], far_b_core[i]], core ^ xorder[i], 1) for i in range(nx)]

    xsub = subsets(xs)
    plan_a = [
        (k ^ x, y ^ z) for k in (0, core) for x in xsub for y in (0, ym) for z in zsub
    ]
    plan_b = [
        (k ^ x, y ^ z) for k in (0, core) for y in (0, ym) for x in xsub for z in zsub
    ]
    steps_a = [(m, 0) for m in reversed(xs)] + [(0, ym)]
    steps_b = [(0, ym)] + [(m, 0) for m in reversed(xs)]
    finish = (nctx, tok, eorder, (plan_a, plan_b))
    lhs_a, lhs_b = experts(idx, third, router, weights, width, g2, finish)

    outs = []
    hw = width // 2
    for lhs, lo, steps in ((lhs_a, 0, steps_a), (lhs_b, hw, steps_b)):
        send, keep = down(lhs, down_v, lo)
        x = keep + swap(send, cm=core).astype(F32)
        for cm, em in steps:
            half = x.shape[0] // 2
            got = swap(x[half:].astype(BF), cm=cm, em=em)
            x = x[:half] + got.astype(F32)
        outs.append(x)

    parts = attention_parts(idx, att_blk, nctx, tok)
    parts = [swap(p, cm=k) if k else p for k, p in enumerate(parts)]

    both = jnp.concatenate(outs, axis=1)
    got = [
        swap(both[i * tok : (i + 1) * tok].astype(BF), em=m)
        for i, m in enumerate(zsub)
        if m
    ]
    return finalize(idx, residual, parts, both[:tok], got)


FETCHES = ((0, 2), (2, 4), (4, 7), (7, 8))


def solution(mesh):
    return jax.shard_map(
        body,
        mesh=mesh,
        in_specs=(
            P("ctx", "exp", None),
            P("ctx", "exp"),
            P(None, "ctx"),
            P(None, "ctx"),
            P(),
            P("exp", None, None),
            P("exp", "ctx"),
            P(("ctx", "exp"), None),
            P(),
            P(),
            P(("ctx", "exp"), None),
            P("exp", None, "ctx"),
            P("exp", None, "ctx"),
            P("exp", "ctx", None),
        ),
        out_specs=P(("ctx", "exp"), None),
        check_vma=False,
    )
```

time: 270 us -> 115 us (0.43)
  waiting for transfers between devices: 153 us -> 30.5 us
  Pallas kernels: 0 us -> 44.8 us
  blocking collectives: 44.4 us -> 0 us
  matrix products: 30.6 us -> 0 us
  starting transfers between devices: 9.06 us -> 36.6 us
  local copies, waits for them, and re-layouts: 14.2 us -> 0.78 us
  between operations: 13.4 us -> 0.49 us
  other arithmetic: 4.49 us -> 1.34 us
    unnamed x5 -> x0, waiting for transfers between devices: 108 us -> none
    pallas_call x0 -> x17, Pallas kernels: none -> 44.8 us  [call(): pl.pallas_call(kernel, out_shape=tuple(shapes), in_specs=[pl.BlockSpec(me...]
    ppermute x0 -> x39, starting transfers between devices: none -> 36.6 us  [swap(): lax.ppermute(x, ('ctx', 'exp'), [(i, i ^ m) for i in range(nctx * nexp)])]
    dot_general x11 -> x0, matrix products: 30.6 us -> none  [the longest x1 8.57 us: body(): jnp.einsum('end,edf->enf', portion, w_gate, preferred_element_type=jnp.fl...]
    ppermute x0 -> x39, waiting for transfers between devices: none -> 30.5 us  [swap(): lax.ppermute(x, ('ctx', 'exp'), [(i, i ^ m) for i in range(nctx * nexp)])]
    all_to_all x1 -> x0, blocking collectives: 26.9 us -> none  [body(): lax.all_to_all(send_rows.reshape(expert_count, CAP, model_width), 'exp',...]
    all_gather x1 -> x0, waiting for transfers between devices: 23.9 us -> none  [body(): portion = lax.all_gather(arrived, 'ctx', axis=1, tiled=True)]
    all_to_all x2 -> x0, waiting for transfers between devices: 20.6 us -> none  [the longest x1 17.2 us: body(): lax.all_to_all(going_back, 'exp', split_axis=0, concat_axis=2, tiled=True)]
  transfers between devices with their start and end apart: 5 -> 39, of which waited for: 5 -> 14; matrix products, arithmetic and copies ran while one was open for 1% -> 2% of each run, Pallas kernels for 0% -> 27%
where the time goes in v1:
time: 115 us
  Pallas kernels  44.8 us (39%)
  starting transfers between devices  36.6 us (32%)
  waiting for transfers between devices  30.5 us (27%)
  other arithmetic  1.34 us (1%)
    pallas_call x17, Pallas kernels, call(): pl.pallas_call(kernel, out_shape=tuple(shapes), in_specs=[pl.BlockSpec(me...  44.8 us
    ppermute x39, starting transfers between devices, swap(): lax.ppermute(x, ('ctx', 'exp'), [(i, i ^ m) for i in range(nctx * nexp)])  36.6 us
    ppermute x39, waiting for transfers between devices, swap(): lax.ppermute(x, ('ctx', 'exp'), [(i, i ^ m) for i in range(nctx * nexp)])  30.5 us
  transfers between devices with their start and end apart: 39, of which 14 were waited for; matrix products, arithmetic and copies ran while one was open for 2% of the time, Pallas kernels for 27%

profile of v1, /device:TPU:0, one launch (start us, length us, event | category | flops | bytes accessed | tf_op | source)
XLA Modules:
  0.0 114.5 jit_solution(1347767190264212333)
XLA Ops:
  0.0 3.0 %collective-permute-start.3 = (bf16[576,128]{1,0:T(8,128)(2,1)}, bf16[576,128]{1,0:T(8,128)(2,1)S(1)}, u32[]{:S(2)}, u32[]{:S(2)}) collective-permute-start(bf16[576,128]{1,0:T(8,128)(2,1)} %refs_0_.2), channel_id=1, source_target_pairs={{0,16},{1,17},{2,18},{3,19},{4,20},{5,21},{6,22},{7,23},{8,24},{9,... | collective-permute-start | bytes 442376 | tf_op jit(solution)/shard_map/ppermute | solution.py:538
  3.5 4.0 %collective-permute-done.3.refs_4_ = bf16[576,128]{1,0:T(8,128)(2,1)S(1)} collective-permute-done((bf16[576,128]{1,0:T(8,128)(2,1)}, bf16[576,128]{1,0:T(8,128)(2,1)S(1)}, u32[]{:S(2)}, u32[]{:S(2)}) %collective-permute-start.3) | collective-permute-done | bytes 147488 | tf_op jit(solution)/shard_map/ppermute | solution.py:538
  10.9 4.9 %shard_map.138 = (bf16[32,2048]{1,0:T(8,128)(2,1)S(1)}, bf16[2048,1792]{1,0:T(8,128)(2,1)S(1)}) custom-call(s32[10]{0:T(128)S(1)} %pad_add_fusion.1.refs_0_, bf16[512,512]{1,0:T(8,128)(2,1)S(1)} %bitcast.46, bf16[512,64]{1,0:T(8,128)(2,1)S(1)} %bitcast.47, bf16[576,128]{1,0:T(8,128)(2,1)S(1)} %get-tuple-element.56.refs_3_, ...), custom_call_target="tpu_custom_call" | custom-call | flops 713031680 | tf_op jit(solution)/shard_map/pallas_call | solution.py:57
  15.8 1.8 %collective-permute-start.9 = (bf16[32,2048]{1,0:T(8,128)(2,1)S(1)}, bf16[32,2048]{1,0:T(8,128)(2,1)S(1)}, u32[]{:S(2)}, u32[]{:S(2)}) collective-permute-start(bf16[32,2048]{1,0:T(8,128)(2,1)S(1)} %get-tuple-element.58.refs_0_), channel_id=1, source_target_pairs={{0,16},{1,17},{2,18},{3,19},{4,20},{5,21},{6,22},{7,23},{8,24},{9,... | collective-permute-start | bytes 393224 | tf_op jit(solution)/shard_map/ppermute | solution.py:538
  17.6 3.7 %collective-permute-done.9.refs_1_ = bf16[32,2048]{1,0:T(8,128)(2,1)S(1)} collective-permute-done((bf16[32,2048]{1,0:T(8,128)(2,1)S(1)}, bf16[32,2048]{1,0:T(8,128)(2,1)S(1)}, u32[]{:S(2)}, u32[]{:S(2)}) %collective-permute-start.9) | collective-permute-done | bytes 131104 | tf_op jit(solution)/shard_map/ppermute | solution.py:538
  22.7 1.9 %shard_map.139 = (bf16[64,1792]{1,0:T(8,128)(2,1)S(1)}, f32[64,1792]{1,0:T(8,128)S(1)}) custom-call(s32[2]{0:T(128)S(1)} %pad_add_fusion.idx_ref.refs_0_, bf16[32,2048]{1,0:T(8,128)(2,1)S(1)} %get-tuple-element.58.refs_0_, bf16[32,2048]{1,0:T(8,128)(2,1)S(1)} %collective-permute-done.9.refs_1_, bf16[32,2048]{1,0:T(8,128)(2,1)S(1)} %collective-permute-done.10.refs_2_, ...), custom_call_target="tpu_custom_call" | custom-call | flops 939524096 | tf_op jit(solution)/shard_map/pallas_call | solution.py:57
  24.6 1.8 %collective-permute-start.12 = (bf16[64,1792]{1,0:T(8,128)(2,1)S(1)}, bf16[64,1792]{1,0:T(8,128)(2,1)S(1)}, u32[]{:S(2)}, u32[]{:S(2)}) collective-permute-start(bf16[64,1792]{1,0:T(8,128)(2,1)S(1)} %get-tuple-element.61), channel_id=1, source_target_pairs={{0,1},{1,0},{2,3},{3,2},{4,5},{5,4},{6,7},{7,6},{8,9},{9,8},{10,11... | collective-permute-start | bytes 688136 | tf_op jit(solution)/shard_map/ppermute | solution.py:538
  29.0 4.3 %shard_map.145 = (f32[8,128]{1,0:T(8,128)}, bf16[2,896,512]{2,1,0:T(8,128)(2,1)S(1)}, bf16[2,896,512]{2,1,0:T(8,128)(2,1)S(1)}, bf16[2,896,512]{2,1,0:T(8,128)(2,1)S(1)}, bf16[2,896,512]{2,1,0:T(8,128)(2,1)S(1)}) custom-call(s32[2]{0:T(128)S(1)} %pad_add_fusion.idx_ref.refs_0_, bf16[2,7168,512]{2,1,0:T(8,128)(2,1)} %wg_ref.7, bf16[2,7168,512]{2,1,0:T(8,128)(2,1)} %wu_ref.7), custom_call_target="tpu_custom_call" | custom-call | flops 1073741824 | tf_op jit(solution)/shard_map/pallas_call | solution.py:57
  33.3 4.3 %shard_map.144 = (f32[8,128]{1,0:T(8,128)}, bf16[2,896,512]{2,1,0:T(8,128)(2,1)S(1)}, bf16[2,896,512]{2,1,0:T(8,128)(2,1)S(1)}, bf16[2,896,512]{2,1,0:T(8,128)(2,1)S(1)}, bf16[2,896,512]{2,1,0:T(8,128)(2,1)S(1)}) custom-call(s32[2]{0:T(128)S(1)} %pad_add_fusion.idx_ref.refs_0_, bf16[2,7168,512]{2,1,0:T(8,128)(2,1)} %wg_ref.7, bf16[2,7168,512]{2,1,0:T(8,128)(2,1)} %wu_ref.7), custom_call_target="tpu_custom_call" | custom-call | flops 1073741824 | tf_op jit(solution)/shard_map/pallas_call | solution.py:57
  37.8 1.6 %collective-permute-start.13 = (bf16[16,1792]{1,0:T(8,128)(2,1)S(1)}, bf16[16,1792]{1,0:T(8,128)(2,1)S(1)}, u32[]{:S(2)}, u32[]{:S(2)}) collective-permute-start(bf16[16,1792]{1,0:T(8,128)(2,1)S(1)} %get-tuple-element.116), channel_id=1, source_target_pairs={{0,2},{1,3},{2,0},{3,1},{4,6},{5,7},{6,4},{7,5},{8,10},{9,11},{10,... | collective-permute-start | bytes 172040 | tf_op jit(solution)/shard_map/ppermute | solution.py:538
  39.4 2.6 %collective-permute-start.14 = (bf16[16,1792]{1,0:T(8,128)(2,1)S(1)}, bf16[16,1792]{1,0:T(8,128)(2,1)S(1)}, u32[]{:S(2)}, u32[]{:S(2)}) collective-permute-start(bf16[16,1792]{1,0:T(8,128)(2,1)S(1)} %get-tuple-element.115), channel_id=1, source_target_pairs={{0,4},{1,5},{2,6},{3,7},{4,0},{5,1},{6,2},{7,3},{8,12},{9,13},{10,... | collective-permute-start | bytes 172040 | tf_op jit(solution)/shard_map/ppermute | solution.py:538
  42.2 5.4 %shard_map.142 = (f32[8,128]{1,0:T(8,128)}, bf16[2,896,512]{2,1,0:T(8,128)(2,1)S(1)}, bf16[2,896,512]{2,1,0:T(8,128)(2,1)S(1)}, bf16[2,896,512]{2,1,0:T(8,128)(2...) custom-call(s32[2]{0:T(128)S(1)} %pad_add_fusion.idx_ref.refs_0_, ...), custom_call_target="tpu_custom_call" | custom-call | flops 1073741824 | tf_op jit(solution)/shard_map/pallas_call | solution.py:57
  50.3 2.0 %collective-permute-start.21 = (bf16[16,1920]{1,0:T(8,128)(2,1)S(1)}, bf16[16,1920]{1,0:T(8,128)(2,1)S(1)}, u32[]{:S(2)}, u32[]{:S(2)}) collective-permute-start(bf16[16,1920]{1,0:T(8,128)(2,1)S(1)} %get-tuple-element.67), channel_id=1, source_target_pairs={{0,6},{1,7},{2,4},{3,5},{4,2},{5,3},{6,0},{7,1},{8,14},{9,15},{10,... | collective-permute-start | bytes 184328 | tf_op jit(solution)/shard_map/ppermute | solution.py:538
  52.8 3.2 %shard_map.143 = (f32[8,128]{1,0:T(8,128)}, bf16[2,896,512]{2,1,0:T(8,128)(2,1)S(1)}, bf16[2,896,512]{2,1,0:T(8,128)(2,1)S(1)}) custom-call(s32[2]{0:T(128)S(1)} %pad_add_fusion.idx_ref.refs_0_, bf16[2,7168,512]{2,1,0:T(8,128)(2,1)} %wg_ref.7, bf16[2,7168,512]{2,1,0:T(8,128)(2,1)} %wu_ref.7), custom_call_target="tpu_custom_call" | custom-call | flops 1073741824 | tf_op jit(solution)/shard_map/pallas_call | solution.py:57
  59.3 2.7 %collective-permute-done.26 = bf16[1,64,896]{2,1,0:T(8,128)(2,1)S(1)} collective-permute-done((bf16[1,64,896]{2,1,0:T(8,128)(2,1)S(1)}, bf16[1,64,896]{2,1,0:T(8,128)(2,1)S(1)}, u32[]{:S(2)}, u32[]{:S(2)}) %collective-permute-start.26) | collective-permute-done | bytes 114720 | tf_op jit(solution)/shard_map/ppermute | solution.py:538
  62.6 5.8 %shard_map.149 = (f32[8,128]{1,0:T(8,128)}, bf16[2,512,7168]{2,1,0:T(8,128)(2,1)S(1)}) custom-call(bf16[2,512,7168]{2,1,0:T(8,128)(2,1)} %refs_0_.3), custom_call_target="tpu_custom_call" | custom-call | flops 1073741824 | tf_op jit(solution)/shard_map/pallas_call | solution.py:57
  72.0 5.3 %collective-permute-done.24 = bf16[1,128,1024]{2,1,0:T(8,128)(2,1)S(1)} collective-permute-done((bf16[1,128,1024]{2,1,0:T(8,128)(2,1)S(1)}, bf16[1,128,1024]{2,1,0:T(8,128)(2,1)S(1)}, u32[]{:S(2)}, u32[]{:S(2)}) %collective-permute-start.24) | collective-permute-done | bytes 262176 | tf_op jit(solution)/shard_map/ppermute | solution.py:538
  77.3 2.5 %shard_map.147 = (f32[2,128,512]{2,1,0:T(8,128)S(1)}, f32[2,128,512]{2,1,0:T(8,128)S(1)}, f32[128,16]{1,0:T(8,128)S(1)}, f32[128,1]{1,0:T(8,128)S(1)}) custom-call(s32[2]{0:T(128)S(1)} %pad_add_fusion.idx_ref.refs_0_, bf16[128,1024]{1,0:T(8,128)(2,1)S(1)} %bitcast.51, bf16[64,896]{1,0:T(8,128)(2,1)S(1)} %get-tuple-element.103.refs_2_, ...), custom_call_target="tpu_custom_call" | custom-call | flops 1409286144 | tf_op jit(solution)/shard_map/pallas_call | solution.py:57
  79.9 3.5 %shard_map.148 = (bf16[128,1024]{1,0:T(8,128)(2,1)S(1)}, bf16[128,1024]{1,0:T(8,128)(2,1)S(1)}) custom-call(s32[2]{0:T(128)S(1)} %pad_add_fusion.idx_ref.refs_0_, bf16[128,1024]{1,0:T(8,128)(2,1)S(1)} %bitcast.49, bf16[128,1024]{1,0:T(8,128)(2,1)S(1)} %bitcast.50, bf16[64,896]{1,0:T(8,128)(2,1)S(1)} %get-tuple-element.113.refs_3_, ...), custom_call_target="tpu_custom_call" | custom-call | flops 1879048192 | tf_op jit(solution)/shard_map/pallas_call | solution.py:57
  93.2 4.5 %collective-permute-done.34 = bf16[32,3584]{1,0:T(8,128)(2,1)S(1)} collective-permute-done((bf16[32,3584]{1,0:T(8,128)(2,1)S(1)}, bf16[32,3584]{1,0:T(8,128)(2,1)S(1)}, u32[]{:S(2)}, u32[]{:S(2)}) %collective-permute-start.34) | collective-permute-done | bytes 229408 | tf_op jit(solution)/shard_map/ppermute | solution.py:538
  102.6 1.7 %collective-permute-done.32 = bf16[16,3584]{1,0:T(8,128)(2,1)S(1)} collective-permute-done((bf16[16,3584]{1,0:T(8,128)(2,1)S(1)}, bf16[16,3584]{1,0:T(8,128)(2,1)S(1)}, u32[]{:S(2)}, u32[]{:S(2)}) %collective-permute-start.32) | collective-permute-done | bytes 114720 | tf_op jit(solution)/shard_map/ppermute | solution.py:538
  105.2 2.1 %collective-permute-start.37 = (bf16[4,7168]{1,0:T(4,128)(2,1)S(1)}, bf16[4,7168]{1,0:T(4,128)(2,1)S(1)}, u32[]{:S(2)}, u32[]{:S(2)}) collective-permute-start(bf16[4,7168]{1,0:T(4,128)(2,1)S(1)} %get-tuple-element.106), channel_id=1, source_target_pairs={{0,4},{1,5},{2,6},{3,7},{4,0},{5,1},{6,2},{7,3},{8,12},{9,13},{10,... | collective-permute-start | bytes 172040 | tf_op jit(solution)/shard_map/ppermute | solution.py:538
  108.9 2.6 %collective-permute-done.37.refs_6_ = bf16[4,7168]{1,0:T(4,128)(2,1)S(1)} collective-permute-done((bf16[4,7168]{1,0:T(4,128)(2,1)S(1)}, bf16[4,7168]{1,0:T(4,128)(2,1)S(1)}, u32[]{:S(2)}, u32[]{:S(2)}) %collective-permute-start.37) | collective-permute-done | bytes 57376 | tf_op jit(solution)/shard_map/ppermute | solution.py:538
  111.5 1.8 %collective-permute-done.38.refs_7_ = bf16[4,7168]{1,0:T(4,128)(2,1)S(1)} collective-permute-done((bf16[4,7168]{1,0:T(4,128)(2,1)S(1)}, bf16[4,7168]{1,0:T(4,128)(2,1)S(1)}, u32[]{:S(2)}, u32[]{:S(2)}) %collective-permute-start.38) | collective-permute-done | bytes 57376 | tf_op jit(solution)/shard_map/ppermute | solution.py:538
  (113 shorter events, 37.1 us)
Async XLA Ops:
  0.0 7.5 %collective-permute-start.3 = (bf16[576,128]{1,0:T(8,128)(2,1)}, bf16[576,128]{1,0:T(8,128)(2,1)S(1)}, u32[]{:S(2)}, u32[]{:S(2)}) collective-permute-start(bf16[576,128]{1,0:T(8,128)(2,1)} %refs_0_.2), channel_id=1, source_target_pairs={{0,16},{1,17},{2,18},{3,19},{4,20},{5,21},{6,22},{7,23},{8,24},{9,... | collective-permute-start | bytes 442376 | tf_op jit(solution)/shard_map/ppermute | solution.py:538
  3.0 7.8 %collective-permute-start.7 = (bf16[32,576]{1,0:T(8,128)(2,1)}, bf16[32,576]{1,0:T(8,128)(2,1)S(1)}, u32[]{:S(2)}, u32[]{:S(2)}) collective-permute-start(bf16[32,576]{1,0:T(8,128)(2,1)} %bitcast.62), channel_id=1, source_target_pairs={{0,8},{1,9},{2,10},{3,11},{4,12},{5,13},{6,14},{7,15},{8,0},{9,1},... | collective-permute-start | bytes 110600 | tf_op jit(solution)/shard_map/ppermute | solution.py:538
  3.0 7.8 %collective-permute-start.4 = (bf16[576,128]{1,0:T(8,128)(2,1)}, bf16[576,128]{1,0:T(8,128)(2,1)S(1)}, u32[]{:S(2)}, u32[]{:S(2)}) collective-permute-start(bf16[576,128]{1,0:T(8,128)(2,1)} %refs_0_.2), channel_id=1, source_target_pairs={{0,8},{1,9},{2,10},{3,11},{4,12},{5,13},{6,14},{7,15},{8,0},{9,1},... | collective-permute-start | bytes 442376 | tf_op jit(solution)/shard_map/ppermute | solution.py:538
  24.6 13.0 %collective-permute-start.12 = (bf16[64,1792]{1,0:T(8,128)(2,1)S(1)}, bf16[64,1792]{1,0:T(8,128)(2,1)S(1)}, u32[]{:S(2)}, u32[]{:S(2)}) collective-permute-start(bf16[64,1792]{1,0:T(8,128)(2,1)S(1)} %get-tuple-element.61), channel_id=1, source_target_pairs={{0,1},{1,0},{2,3},{3,2},{4,5},{5,4},{6,7},{7,6},{8,9},{9,8},{10,11... | collective-permute-start | bytes 688136 | tf_op jit(solution)/shard_map/ppermute | solution.py:538
  27.1 14.9 %collective-permute-start = (bf16[4,1920]{1,0:T(4,128)(2,1)S(1)}, bf16[4,1920]{1,0:T(4,128)(2,1)S(1)}, u32[]{:S(2)}, u32[]{:S(2)}) collective-permute-start(bf16[4,1920]{1,0:T(4,128)(2,1)S(1)} %get-tuple-element.53), channel_id=1, source_target_pairs={{0,8},{1,9},{2,10},{3,11},{4,12},{5,13},{6,14},{7,15},{8,0},{9,1},... | collective-permute-start | bytes 46088 | tf_op jit(solution)/shard_map/ppermute | solution.py:538
  27.2 20.5 %collective-permute-start.1 = (bf16[4,1920]{1,0:T(4,128)(2,1)S(1)}, bf16[4,1920]{1,0:T(4,128)(2,1)S(1)}, u32[]{:S(2)}, u32[]{:S(2)}) collective-permute-start(bf16[4,1920]{1,0:T(4,128)(2,1)S(1)} %get-tuple-element.54), channel_id=1, source_target_pairs={{0,16},{1,17},{2,18},{3,19},{4,20},{5,21},{6,22},{7,23},{8,24},{9,... | collective-permute-start | bytes 46088 | tf_op jit(solution)/shard_map/ppermute | solution.py:538
  28.7 19.0 %collective-permute-start.2 = (bf16[4,1920]{1,0:T(4,128)(2,1)S(1)}, bf16[4,1920]{1,0:T(4,128)(2,1)S(1)}, u32[]{:S(2)}, u32[]{:S(2)}) collective-permute-start(bf16[4,1920]{1,0:T(4,128)(2,1)S(1)} %get-tuple-element.55), channel_id=1, source_target_pairs={{0,24},{1,25},{2,26},{3,27},{4,28},{5,29},{6,30},{7,31},{8,16},{9,... | collective-permute-start | bytes 46088 | tf_op jit(solution)/shard_map/ppermute | solution.py:538
  37.8 9.9 %collective-permute-start.13 = (bf16[16,1792]{1,0:T(8,128)(2,1)S(1)}, bf16[16,1792]{1,0:T(8,128)(2,1)S(1)}, u32[]{:S(2)}, u32[]{:S(2)}) collective-permute-start(bf16[16,1792]{1,0:T(8,128)(2,1)S(1)} %get-tuple-element.116), channel_id=1, source_target_pairs={{0,2},{1,3},{2,0},{3,1},{4,6},{5,7},{6,4},{7,5},{8,10},{9,11},{10,... | collective-permute-start | bytes 172040 | tf_op jit(solution)/shard_map/ppermute | solution.py:538
  39.4 8.3 %collective-permute-start.14 = (bf16[16,1792]{1,0:T(8,128)(2,1)S(1)}, bf16[16,1792]{1,0:T(8,128)(2,1)S(1)}, u32[]{:S(2)}, u32[]{:S(2)}) collective-permute-start(bf16[16,1792]{1,0:T(8,128)(2,1)S(1)} %get-tuple-element.115), channel_id=1, source_target_pairs={{0,4},{1,5},{2,6},{3,7},{4,0},{5,1},{6,2},{7,3},{8,12},{9,13},{10,... | collective-permute-start | bytes 172040 | tf_op jit(solution)/shard_map/ppermute | solution.py:538
  42.0 6.0 %collective-permute-start.15 = (bf16[16,1792]{1,0:T(8,128)(2,1)S(1)}, bf16[16,1792]{1,0:T(8,128)(2,1)S(1)}, u32[]{:S(2)}, u32[]{:S(2)}) collective-permute-start(bf16[16,1792]{1,0:T(8,128)(2,1)S(1)} %get-tuple-element.114), channel_id=1, source_target_pairs={{0,6},{1,7},{2,4},{3,5},{4,2},{5,3},{6,0},{7,1},{8,14},{9,15},{10,... | collective-permute-start | bytes 172040 | tf_op jit(solution)/shard_map/ppermute | solution.py:538
  48.8 7.2 %collective-permute-start.20 = (bf16[16,1920]{1,0:T(8,128)(2,1)S(1)}, bf16[16,1920]{1,0:T(8,128)(2,1)S(1)}, u32[]{:S(2)}, u32[]{:S(2)}) collective-permute-start(bf16[16,1920]{1,0:T(8,128)(2,1)S(1)} %get-tuple-element.67), channel_id=1, source_target_pairs={{0,4},{1,5},{2,6},{3,7},{4,0},{5,1},{6,2},{7,3},{8,12},{9,13},{10,... | collective-permute-start | bytes 184328 | tf_op jit(solution)/shard_map/ppermute | solution.py:538
  50.3 6.3 %collective-permute-start.21 = (bf16[16,1920]{1,0:T(8,128)(2,1)S(1)}, bf16[16,1920]{1,0:T(8,128)(2,1)S(1)}, u32[]{:S(2)}, u32[]{:S(2)}) collective-permute-start(bf16[16,1920]{1,0:T(8,128)(2,1)S(1)} %get-tuple-element.67), channel_id=1, source_target_pairs={{0,6},{1,7},{2,4},{3,5},{4,2},{5,3},{6,0},{7,1},{8,14},{9,15},{10,... | collective-permute-start | bytes 184328 | tf_op jit(solution)/shard_map/ppermute | solution.py:538
  58.7 9.8 %collective-permute-start.22 = (bf16[1,64,1024]{2,1,0:T(8,128)(2,1)S(1)}, bf16[1,64,1024]{2,1,0:T(8,128)(2,1)S(1)}, u32[]{:S(2)}, u32[]{:S(2)}) collective-permute-start(bf16[1,64,1024]{2,1,0:T(8,128)(2,1)S(1)} %slice_bitcast_fusion), channel_id=1, source_target_pairs={{0,1},{1,0},{2,3},{3,2},{4,5},{5,4},{6,7},{7,6},{8,9},{9,8},{10,11... | collective-permute-start | bytes 393224 | tf_op jit(solution)/shard_map/ppermute | solution.py:538
  62.0 9.6 %collective-permute-start.28 = (bf16[2,64,896]{2,1,0:T(8,128)(2,1)S(1)}, bf16[2,64,896]{2,1,0:T(8,128)(2,1)S(1)}, u32[]{:S(2)}, u32[]{:S(2)}) collective-permute-start(bf16[2,64,896]{2,1,0:T(8,128)(2,1)S(1)} %pad_maximum_fusion.3), channel_id=1, source_target_pairs={{0,1},{1,0},{2,3},{3,2},{4,5},{5,4},{6,7},{7,6},{8,9},{9,8},{10,11... | collective-permute-start | bytes 688136 | tf_op jit(solution)/shard_map/ppermute | solution.py:538
  68.5 8.8 %collective-permute-start.24 = (bf16[1,128,1024]{2,1,0:T(8,128)(2,1)S(1)}, bf16[1,128,1024]{2,1,0:T(8,128)(2,1)S(1)}, u32[]{:S(2)}, u32[]{:S(2)}) collective-permute-start(bf16[1,128,1024]{2,1,0:T(8,128)(2,1)S(1)} %get-tuple-element.102), channel_id=1, source_target_pairs={{0,16},{1,17},{2,18},{3,19},{4,20},{5,21},{6,22},{7,23},{8,24},{9,... | collective-permute-start | bytes 786440 | tf_op jit(solution)/shard_map/ppermute | solution.py:538
  70.1 9.8 %collective-permute-start.23 = (bf16[1,128,1024]{2,1,0:T(8,128)(2,1)S(1)}, bf16[1,128,1024]{2,1,0:T(8,128)(2,1)S(1)}, u32[]{:S(2)}, u32[]{:S(2)}) collective-permute-start(bf16[1,128,1024]{2,1,0:T(8,128)(2,1)S(1)} %get-tuple-element.102), channel_id=1, source_target_pairs={{0,8},{1,9},{2,10},{3,11},{4,12},{5,13},{6,14},{7,15},{8,0},{9,1},... | collective-permute-start | bytes 786440 | tf_op jit(solution)/shard_map/ppermute | solution.py:538
  71.6 8.2 %collective-permute-start.29 = (bf16[2,64,896]{2,1,0:T(8,128)(2,1)S(1)}, bf16[2,64,896]{2,1,0:T(8,128)(2,1)S(1)}, u32[]{:S(2)}, u32[]{:S(2)}) collective-permute-start(bf16[2,64,896]{2,1,0:T(8,128)(2,1)S(1)} %collective-permute-done.28), channel_id=1, source_target_pairs={{0,8},{1,9},{2,10},{3,11},{4,12},{5,13},{6,14},{7,15},{8,0},{9,1},... | collective-permute-start | bytes 688136 | tf_op jit(solution)/shard_map/ppermute | solution.py:538
  86.2 21.1 %collective-permute-start.16 = (bf16[4,1792]{1,0:T(4,128)(2,1)S(1)}, bf16[4,1792]{1,0:T(4,128)(2,1)S(1)}, u32[]{:S(2)}, u32[]{:S(2)}) collective-permute-start(bf16[4,1792]{1,0:T(4,128)(2,1)S(1)} %get-tuple-element.64), channel_id=1, source_target_pairs={{0,8},{1,9},{2,10},{3,11},{4,12},{5,13},{6,14},{7,15},{8,0},{9,1},... | collective-permute-start | bytes 43016 | tf_op jit(solution)/shard_map/ppermute | solution.py:538
  86.3 22.6 %collective-permute-start.17 = (bf16[4,1792]{1,0:T(4,128)(2,1)S(1)}, bf16[4,1792]{1,0:T(4,128)(2,1)S(1)}, u32[]{:S(2)}, u32[]{:S(2)}) collective-permute-start(bf16[4,1792]{1,0:T(4,128)(2,1)S(1)} %get-tuple-element.65), channel_id=1, source_target_pairs={{0,16},{1,17},{2,18},{3,19},{4,20},{5,21},{6,22},{7,23},{8,24},{9,... | collective-permute-start | bytes 43016 | tf_op jit(solution)/shard_map/ppermute | solution.py:538
  87.8 21.1 %collective-permute-start.18 = (bf16[4,1792]{1,0:T(4,128)(2,1)S(1)}, bf16[4,1792]{1,0:T(4,128)(2,1)S(1)}, u32[]{:S(2)}, u32[]{:S(2)}) collective-permute-start(bf16[4,1792]{1,0:T(4,128)(2,1)S(1)} %get-tuple-element.66), channel_id=1, source_target_pairs={{0,24},{1,25},{2,26},{3,27},{4,28},{5,29},{6,30},{7,31},{8,16},{9,... | collective-permute-start | bytes 43016 | tf_op jit(solution)/shard_map/ppermute | solution.py:538
  89.9 7.7 %collective-permute-start.34 = (bf16[32,3584]{1,0:T(8,128)(2,1)S(1)}, bf16[32,3584]{1,0:T(8,128)(2,1)S(1)}, u32[]{:S(2)}, u32[]{:S(2)}) collective-permute-start(bf16[32,3584]{1,0:T(8,128)(2,1)S(1)} %slice.153), channel_id=1, source_target_pairs={{0,1},{1,0},{2,3},{3,2},{4,5},{5,4},{6,7},{7,6},{8,9},{9,8},{10,11... | collective-permute-start | bytes 688136 | tf_op jit(solution)/shard_map/ppermute | solution.py:538
  91.6 7.7 %collective-permute-start.31 = (bf16[32,3584]{1,0:T(8,128)(2,1)S(1)}, bf16[32,3584]{1,0:T(8,128)(2,1)S(1)}, u32[]{:S(2)}, u32[]{:S(2)}) collective-permute-start(bf16[32,3584]{1,0:T(8,128)(2,1)S(1)} %slice.154), channel_id=1, source_target_pairs={{0,16},{1,17},{2,18},{3,19},{4,20},{5,21},{6,22},{7,23},{8,24},{9,... | collective-permute-start | bytes 688136 | tf_op jit(solution)/shard_map/ppermute | solution.py:538
  105.2 6.3 %collective-permute-start.37 = (bf16[4,7168]{1,0:T(4,128)(2,1)S(1)}, bf16[4,7168]{1,0:T(4,128)(2,1)S(1)}, u32[]{:S(2)}, u32[]{:S(2)}) collective-permute-start(bf16[4,7168]{1,0:T(4,128)(2,1)S(1)} %get-tuple-element.106), channel_id=1, source_target_pairs={{0,4},{1,5},{2,6},{3,7},{4,0},{5,1},{6,2},{7,3},{8,12},{9,13},{10,... | collective-permute-start | bytes 172040 | tf_op jit(solution)/shard_map/ppermute | solution.py:538
  107.3 6.0 %collective-permute-start.38 = (bf16[4,7168]{1,0:T(4,128)(2,1)S(1)}, bf16[4,7168]{1,0:T(4,128)(2,1)S(1)}, u32[]{:S(2)}, u32[]{:S(2)}) collective-permute-start(bf16[4,7168]{1,0:T(4,128)(2,1)S(1)} %get-tuple-element.105), channel_id=1, source_target_pairs={{0,6},{1,7},{2,4},{3,5},{4,2},{5,3},{6,0},{7,1},{8,14},{9,15},{10,... | collective-permute-start | bytes 172040 | tf_op jit(solution)/shard_map/ppermute | solution.py:538
  (21 other events, 82.7 us)

commit v2 on v1

--- a/solution.py
+++ b/solution.py
@@ -13,6 +13,7 @@
 NORM_EPS = 1e-06
 EXTRA = 128
 IDS = 16
+GROUP_ROWS = 128
 BF = jnp.bfloat16
 F32 = jnp.float32
 I32 = jnp.int32
@@ -78,18 +79,16 @@
     kd, cache_len = kc[0].shape
     rows = kf[0].shape[0]
     heads, lat, vh = w_uv.shape
-    group = max(1, 128 // rows)
+    group = max(1, min(heads, GROUP_ROWS // rows))
     nblk = meta.shape[0] - 2
 
     def kernel(*refs):
         idx_ref, q_ref, qr_ref = refs[:3]
         kc_ref = refs[3 : 3 + nctx]
         kf_ref = refs[3 + nctx : 3 + 2 * nctx]
-        w_hbm, wo_hbm, out_ref, wo_ref, w_ref, sems = refs[3 + 2 * nctx :]
-        load = pltpu.make_async_copy(w_hbm, w_ref, sems.at[0])
+        w_ref, wo_hbm, out_ref, wo_ref, sem = refs[3 + 2 * nctx :]
+        load = pltpu.make_async_copy(wo_hbm, wo_ref, sem)
         load.start()
-        load_out = pltpu.make_async_copy(wo_hbm, wo_ref, sems.at[1])
-        load_out.start()
         c = idx_ref[0]
         starts = [idx_ref[2 + b] * block_rows for b in range(nblk)]
 
@@ -122,28 +121,41 @@
             acc = acc / total
             hi = acc.astype(BF)
             low = (acc - hi.astype(F32)).astype(BF)
-            if g == 0:
-                load.wait()
             for h in range(group):
                 w = w_ref[g * group + h]
                 a = h * rows
                 v = dot(hi[a : a + rows], w) + dot(low[a : a + rows], w)
                 n = (g * group + h) * vh
                 out_ref[:, n : n + vh] = v.astype(BF)
-        load_out.wait()
-
-    specs = (pltpu.SMEM,) + (pltpu.VMEM,) * (2 + 2 * nctx) + (pltpu.HBM,) * 2
+        load.wait()
+
+    specs = (pltpu.SMEM,) + (pltpu.VMEM,) * (3 + 2 * nctx) + (pltpu.HBM,)
     flops = 2 * heads * rows * nctx * (cache_len + rows) * (kd + lat)
     return call(
         kernel,
         [((rows, heads * vh), BF)],
-        (meta, q, qr, *kc, *kf, w_uv, w_out),
+        (meta, q, qr, *kc, *kf, held(w_uv), w_out),
         specs,
         16,
         flops,
         [w_out.shape],
-        [pltpu.VMEM(w_uv.shape, BF), pltpu.SemaphoreType.DMA((2,))],
-    )
+        [pltpu.SemaphoreType.DMA],
+    )
+
+
+def block_copies(c, blocks, hc, srcs, dsts, sems):
+    copies = []
+    for i, (mask, half) in enumerate(blocks):
+        start = pl.multiple_of(((c ^ mask) * 2 + half) * hc, 16)
+        for j in (0, 1):
+            cp = pltpu.make_async_copy(
+                srcs[j].at[:, pl.ds(start, hc), :],
+                dsts[j].at[:, pl.ds(i * hc, hc), :],
+                sems.at[i, j],
+            )
+            cp.start()
+            copies.append(cp)
+    return copies
 
 
 def project(idx, hg, w_out, korder, emasks, tok):
@@ -229,7 +241,6 @@
 def merge(idx, parts, own, got, gain, tok):
     nctx = len(parts)
     blk, cols = own.shape
-    hc = cols // 2
     n = len(got)
 
     def kernel(idx_ref, *refs):
@@ -260,9 +271,8 @@
         lane = lax.broadcasted_iota(I32, extra.shape, 1)
         extra = jnp.where(lane == 0, hi, jnp.where(lane == 1, mid, extra))
         extra = jnp.where(lane == 2, low, extra)
-        sx_ref[:, :hc] = scaled[:, :hc].astype(BF)
-        sx_ref[:, hc : hc + EXTRA] = extra.astype(BF)
-        sx_ref[:, hc + EXTRA :] = scaled[:, hc:].astype(BF)
+        sx_ref[:, :cols] = scaled.astype(BF)
+        sx_ref[:, cols:] = extra.astype(BF)
 
     return call(
         kernel,
@@ -332,69 +342,60 @@
         self.half = half
 
 
-def grab(arrays):
+def grab(arrays, first=0, rows=None):
     n = len(arrays)
+    shapes = [(rows or a.shape[0],) + a.shape[1:] for a in arrays]
 
     def kernel(*refs):
-        tok_ref = refs[n]
-        sems = refs[2 * n + 1]
+        sems = refs[2 * n]
         copies = []
         for i in range(n):
-            copies.append(pltpu.make_async_copy(refs[i], refs[n + 1 + i], sems.at[i]))
+            src = refs[i].at[pl.ds(first, rows)] if rows else refs[i]
+            copies.append(pltpu.make_async_copy(src, refs[n + i], sems.at[i]))
             copies[-1].start()
-        tok_ref[...] = jnp.zeros(tok_ref.shape, F32)
         for cp in copies:
             cp.wait()
 
-    done, *got = call(
-        kernel,
-        [((8, 128), F32)],
+    return call(
+        kernel,
+        [],
         tuple(arrays),
         (pltpu.HBM,) * n,
         1,
         1 << 30,
-        [a.shape for a in arrays],
+        shapes,
         [pltpu.SemaphoreType.DMA((n,))],
     )
-    return done, got
 
 
 def fetch(idx, blocks, w_gate, w_up, hc):
     local, _, ff = w_gate.shape
     n = len(blocks)
 
-    def kernel(idx_ref, wg_ref, wu_ref, tok_ref, *refs):
-        sems = refs[2 * n]
-        copies = []
-        for i, (mask, half) in enumerate(blocks):
-            start = pl.multiple_of(((idx_ref[0] ^ mask) * 2 + half) * hc, 16)
-            for j, src in enumerate((wg_ref, wu_ref)):
-                cp = pltpu.make_async_copy(
-                    src.at[:, pl.ds(start, hc), :], refs[2 * i + j], sems.at[i, j]
-                )
-                cp.start()
-                copies.append(cp)
-        tok_ref[...] = jnp.zeros(tok_ref.shape, F32)
-        for cp in copies:
+    def kernel(idx_ref, wg_ref, wu_ref, g_ref, u_ref, sems):
+        srcs = (wg_ref, wu_ref)
+        for cp in block_copies(idx_ref[0], blocks, hc, srcs, (g_ref, u_ref), sems):
             cp.wait()
 
-    shape = (local, hc, ff)
-    done, *got = call(
-        kernel,
-        [((8, 128), F32)],
+    shape = (local, n * hc, ff)
+    return call(
+        kernel,
+        [],
         (idx, w_gate, w_up),
         (pltpu.SMEM, pltpu.HBM, pltpu.HBM),
         1,
         1 << 30,
-        [shape] * (2 * n),
+        [shape, shape],
         [pltpu.SemaphoreType.DMA((n, 2))],
     )
-    return done, {b: (got[2 * i], got[2 * i + 1]) for i, b in enumerate(blocks)}
-
-
-def experts(idx, chunks, router, weights, width, carry, finish):
-    loaded = [held(w) for ch in chunks for w in weights[ch.mask, ch.half]]
-    local, hc, ff = loaded[0].shape
+
+
+def experts(idx, chunks, router, groups, width, carry, finish, copy=None):
+    loaded = [held(w) for g in groups for w in g[1:]]
+    sizes = [len(g[0]) for g in groups]
+    assert [b for g in groups for b in g[0]] == [(ch.mask, ch.half) for ch in chunks]
+    local, _, ff = loaded[0].shape
+    hc = router.shape[2]
     nw = len(loaded)
     pieces = [p for ch in chunks for p in ch.pieces]
     total = sum(p.shape[0] for p in chunks[0].pieces)
@@ -409,6 +410,11 @@
         wrefs = refs[2 + n : 2 + n + nw]
         crefs = refs[2 + n + nw : 2 + n + nw + ncarry]
         outs = refs[2 + n + nw + ncarry :]
+        if copy:
+            wd_hbm, *outs, wd_ref, sem = outs
+            src = wd_hbm.at[pl.ds(copy[1], copy[2])]
+            load = pltpu.make_async_copy(src, wd_ref, sem)
+            load.start()
         c = idx_ref[0]
         xs = []
         at = 0
@@ -419,7 +425,7 @@
             at += len(parts)
             x = parts[0] if len(parts) == 1 else jnp.concatenate(parts, axis=0)
             block = (c ^ ch.mask) * 2 + ch.half
-            if ch.half == 0:
+            if ch.half == 1:
                 extra = x[:, hc : hc + EXTRA].astype(F32)
                 lane = lax.broadcasted_iota(I32, extra.shape, 1)
                 ssum = ssum + jnp.sum(jnp.where(lane < 3, extra, 0.0), axis=1, keepdims=True)
@@ -427,14 +433,27 @@
             x = x[:, :hc]
             xs.append(x)
             logit = logit + dot_t(x, r_ref[block])
+        pairs = []
+        at = 0
+        for g, size in enumerate(sizes):
+            part = xs[at : at + size]
+            at += size
+            if hc % 128 == 0 and size > 1:
+                pairs.append((jnp.concatenate(part, axis=1), g, 0, size * hc))
+            else:
+                pairs += [(x, g, i * hc, hc) for i, x in enumerate(part)]
+
+        def product(e, c_i):
+            acc = crefs[c_i][e] if ncarry else None
+            for x, g, lo, size in pairs:
+                part = dot(x, wrefs[2 * g + c_i][e, lo : lo + size, :])
+                acc = part if acc is None else acc + part
+            return acc
+
         if finish is None:
             for e in range(local):
                 for c_i in (0, 1):
-                    acc = crefs[c_i][e] if ncarry else None
-                    for i, x in enumerate(xs):
-                        part = dot(x, wrefs[2 * i + c_i][e])
-                        acc = part if acc is None else acc + part
-                    outs[c_i][e] = acc
+                    outs[c_i][e] = product(e, c_i)
             outs[2][...] = logit
             outs[3][...] = ssum
             return
@@ -444,64 +463,67 @@
         lane = lax.broadcasted_iota(I32, mixing.shape, 1)
         acts = []
         for e in range(local):
-            vals = []
-            for c_i in (0, 1):
-                acc = crefs[c_i][e]
-                for i, x in enumerate(xs):
-                    acc = acc + dot(x, wrefs[2 * i + c_i][e])
-                vals.append(acc * scale)
+            vals = [product(e, c_i) * scale for c_i in (0, 1)]
             mine = idx_ref[1] * local + e
             mix = jnp.sum(jnp.where(lane == mine, mixing, 0.0), axis=1, keepdims=True)
             acts.append((jax.nn.silu(vals[0]) * vals[1] * mix).astype(BF))
         act = jnp.concatenate(acts, axis=1)
-        nctx, tok, order_in, plans = finish
+        nctx, tok, order_in, plan = finish
         r = lax.broadcasted_iota(I32, (total, 1), 0)
-        for plan, out_ref in zip(plans, outs):
-            pos = r // tok
-            cm = pick(pos, [a for a, _ in plan])
-            where_in = [order_in.index(b) for _, b in plan]
-            p = pick(pos, where_in)
-            src = (p * nctx + (c ^ cm)) * tok + r % tok
-            perm = (src == lax.broadcasted_iota(I32, (total, total), 1)).astype(F32).astype(BF)
-            out_ref[...] = dot(perm, act).astype(BF)
+        pos = r // tok
+        cm = pick(pos, [a for a, _ in plan])
+        p = pick(pos, [order_in.index(b) for _, b in plan])
+        src = (p * nctx + (c ^ cm)) * tok + r % tok
+        perm = (src == lax.broadcasted_iota(I32, (total, total), 1)).astype(F32).astype(BF)
+        outs[0][...] = dot(perm, act).astype(BF)
+        if copy:
+            load.wait()
 
     acc_shape = (local, total, ff)
     if finish is None:
         outs = [(acc_shape, F32), (acc_shape, F32), ((total, nexperts), F32), ((total, 1), F32)]
     else:
-        outs = [((total, local * ff), BF), ((total, local * ff), BF)]
+        outs = [((total, local * ff), BF)]
     args = (idx, *pieces, router, *loaded, *carry)
     specs = (pltpu.SMEM,) + (pltpu.VMEM,) * (len(args) - 1)
     flops = len(chunks) * 4 * total * hc * ff * local
-    return call(kernel, outs, args, specs, 8, flops)
-
-
-def down(lhs, w_down, lo):
-    total = lhs.shape[0]
-    local, ff, width = w_down.shape
-    hw = width // 2
-
-    def kernel(x_ref, w_ref, send_ref, keep_ref):
+    loads, scratch = [], []
+    if copy:
+        args += (copy[0],)
+        specs += (pltpu.HBM,)
+        loads = [(copy[2], width)]
+        scratch = [pltpu.SemaphoreType.DMA]
+    return call(kernel, outs, args, specs, 8, flops, loads, scratch)
+
+
+def project_down(lhs, blocks, rows, lo, hi):
+    total, depth = lhs.shape
+    nr = len(rows)
+    size = total // len(blocks)
+
+    def kernel(x_ref, *refs):
+        send_ref, keep_ref = refs[nr:]
         half = total // 2
-        step = hw // 4
-        for i in range(4):
+        x = jnp.concatenate([x_ref[b * size : (b + 1) * size] for b in blocks], axis=0)
+        for at in range(lo, hi, 1024):
+            end = min(at + 1024, hi)
             acc = None
-            for e in range(local):
-                part = dot(
-                    x_ref[:, e * ff : (e + 1) * ff],
-                    w_ref[e, :, lo + i * step : lo + (i + 1) * step],
-                )
+            k = 0
+            for r in range(nr):
+                n = rows[r].shape[0]
+                part = dot(x[:, k : k + n], refs[r][:, at:end])
+                k += n
                 acc = part if acc is None else acc + part
-            send_ref[:, i * step : (i + 1) * step] = acc[half:].astype(BF)
-            keep_ref[:, i * step : (i + 1) * step] = acc[:half]
-
-    return call(
-        kernel,
-        [((total // 2, hw), BF), ((total // 2, hw), F32)],
-        (lhs, held(w_down)),
-        (pltpu.VMEM, pltpu.VMEM),
+            send_ref[:, at - lo : end - lo] = acc[half:].astype(BF)
+            keep_ref[:, at - lo : end - lo] = acc[:half]
+
+    return call(
+        kernel,
+        [((total // 2, hi - lo), BF), ((total // 2, hi - lo), F32)],
+        (lhs, *[held(r) for r in rows]),
+        (pltpu.VMEM,) * (nr + 1),
         8,
-        2 * total * local * ff * hw,
+        2 * total * depth * (hi - lo),
     )
 
 
@@ -556,25 +578,34 @@
     korder = korder + [k ^ core for k in korder]
 
     kf_own = fresh_keys.T
-    kc_v, kf_v = grab((cache_keys, kf_own))[1]
+    kc_v, kf_v, w_uv_v = grab((cache_keys, kf_own, w_uv))
     q = q_nope.transpose(1, 0, 2).reshape(heads_here * rows_here, lat)
     qr = q_rope.reshape(rows_here, heads_here, pe).transpose(1, 0, 2)
     qr = qr.reshape(heads_here * rows_here, pe)
     meta = jnp.concatenate([idx, block_order])
     kc, kf = spread((cache_keys, kf_own))
     kc[0], kf[0] = held(kc_v), held(kf_v)
-    head, w_out_v = attend(meta, q, qr, kc, kf, w_uv, w_out, korder, block_rows)
+    head, w_out_v = attend(meta, q, qr, kc, kf, w_uv_v, w_out, korder, block_rows)
 
     xorder = subsets(xs)
     nx = len(xorder)
-    order = [(m, h) for m in xorder for h in (0, 1)]
-    order = order + [(m ^ core, h) for m, h in order]
-    count = len(order)
-    weights = {}
-    for lo, hi in FETCHES:
-        part = order[count * lo // 8 : count * hi // 8]
-        weights.update(fetch(idx, part, w_gate, w_up, hc)[1])
-    down_v = grab((w_down,))[1][0]
+    blocks_1 = [(0, 0)]
+    blocks_2 = [(m, 0) for m in xorder[1:]] + [(m, 1) for m in xorder]
+    blocks_3 = [(m ^ core, h) for m, h in blocks_1 + blocks_2]
+
+    def load(blocks):
+        return (blocks, *fetch(idx, blocks, w_gate, w_up, hc))
+
+    cut = len(blocks_2) * 2 // 3
+    quarter = len(blocks_3) // 4
+    groups_1 = [load(blocks_1)]
+    groups_2 = [load(blocks_2[:cut]), load(blocks_2[cut:])]
+    groups_3 = [load(blocks_3[: 2 * quarter])]
+    groups_3 += [load(blocks_3[2 * quarter :])]
+    w_down = w_down.reshape(-1, width)
+    dq = w_down.shape[0] // 4
+    down_v = grab((w_down,), 0, dq)
+    down_v += grab((w_down,), dq, 2 * dq)
 
     res_got = residual_parts(idx, residual, expert_ids, nctx)
     res_got = [swap(p, cm=k) if k else p for k, p in enumerate(res_got)]
@@ -593,8 +624,8 @@
 
     zx = jnp.stack([swap(sx, em=m) if m else sx for m in zsub])
     zx = zx.reshape(len(zsub) * blk, -1)
-    za = zx[:, : hc + EXTRA][None]
-    zb = zx[:, hc + EXTRA :][None]
+    za = zx[:, :hc][None]
+    zb = zx[:, hc:][None]
     own_a = jnp.concatenate([za, swap(za, em=ym)], axis=1)
     xb = zb
     for m in xs:
@@ -611,10 +642,10 @@
 
     router = router_weight.reshape(2 * nctx, hc, nexperts).transpose(0, 2, 1)
     first = [Chunk([own_a[0]], 0, 0)]
-    g1 = experts(idx, first, router, weights, width, (), None)
+    g1 = experts(idx, first, router, groups_1, width, (), None)
     second = [Chunk([rest_a[i - 1]], xorder[i], 0) for i in range(1, nx)]
     second += [Chunk([xb[i], far_b[i]], xorder[i], 1) for i in range(nx)]
-    g2 = experts(idx, second, router, weights, width, g1, None)
+    g2 = experts(idx, second, router, groups_2, width, g1, None)
     third = [Chunk([own_a_core[0]], core, 0)]
     third += [Chunk([rest_a_core[i - 1]], core ^ xorder[i], 0) for i in range(1, nx)]
     third += [Chunk([xb_core[i], far_b_core[i]], core ^ xorder[i], 1) for i in range(nx)]
@@ -623,18 +654,21 @@
     plan_a = [
         (k ^ x, y ^ z) for k in (0, core) for x in xsub for y in (0, ym) for z in zsub
     ]
-    plan_b = [
-        (k ^ x, y ^ z) for k in (0, core) for y in (0, ym) for x in xsub for z in zsub
-    ]
+    size_x = len(xsub)
+    blocks_a = list(range(4 * size_x))
+    blocks_b = [(k * size_x + x) * 2 + y for k in (0, 1) for y in (0, 1) for x in range(size_x)]
     steps_a = [(m, 0) for m in reversed(xs)] + [(0, ym)]
     steps_b = [(0, ym)] + [(m, 0) for m in reversed(xs)]
-    finish = (nctx, tok, eorder, (plan_a, plan_b))
-    lhs_a, lhs_b = experts(idx, third, router, weights, width, g2, finish)
+    finish = (nctx, tok, eorder, plan_a)
+    last = (w_down, 3 * dq, dq)
+    lhs, down_2 = experts(idx, third, router, groups_3, width, g2, finish, last)
+    down_v.append(down_2)
 
     outs = []
     hw = width // 2
-    for lhs, lo, steps in ((lhs_a, 0, steps_a), (lhs_b, hw, steps_b)):
-        send, keep = down(lhs, down_v, lo)
+    halves = ((blocks_a, 0, hw, steps_a), (blocks_b, hw, width, steps_b))
+    for blocks, lo, hi, steps in halves:
+        send, keep = project_down(lhs, blocks, down_v, lo, hi)
         x = keep + swap(send, cm=core).astype(F32)
         for cm, em in steps:
             half = x.shape[0] // 2
@@ -652,9 +686,6 @@
         if m
     ]
     return finalize(idx, residual, parts, both[:tok], got)
-
-
-FETCHES = ((0, 2), (2, 4), (4, 7), (7, 8))
 
 
 def solution(mesh):

time: 115 us -> 108 us (0.939)
  Pallas kernels: 44.8 us -> 41.7 us
  waiting for transfers between devices: 30.5 us -> 27.7 us
  starting transfers between devices: 36.6 us -> 34.9 us
    pallas_call x17 -> x19, Pallas kernels: 44.8 us -> 41.7 us  [call(): pl.pallas_call(kernel, out_shape=tuple(shapes), in_specs=[pl.BlockSpec(me...]
    ppermute x39, waiting for transfers between devices: 30.5 us -> 27.7 us  [swap(): lax.ppermute(x, ('ctx', 'exp'), [(i, i ^ m) for i in range(nctx * nexp)])]
    ppermute x39, starting transfers between devices: 36.6 us -> 34.9 us  [swap(): lax.ppermute(x, ('ctx', 'exp'), [(i, i ^ m) for i in range(nctx * nexp)])]
  transfers between devices with their start and end apart: 39 -> 39, of which waited for: 14 -> 12; matrix products, arithmetic and copies ran while one was open for 2% -> 3% of each run, Pallas kernels for 27% -> 29%
where the time goes in v2:
time: 108 us
  Pallas kernels  41.7 us (39%)
  starting transfers between devices  34.9 us (32%)
  waiting for transfers between devices  27.7 us (26%)
  local copies, waits for them, and re-layouts  1.63 us (2%)
  other arithmetic  1.3 us (1%)
    pallas_call x19, Pallas kernels, call(): pl.pallas_call(kernel, out_shape=tuple(shapes), in_specs=[pl.BlockSpec(me...  41.7 us
    ppermute x39, starting transfers between devices, swap(): lax.ppermute(x, ('ctx', 'exp'), [(i, i ^ m) for i in range(nctx * nexp)])  34.9 us
    ppermute x39, waiting for transfers between devices, swap(): lax.ppermute(x, ('ctx', 'exp'), [(i, i ^ m) for i in range(nctx * nexp)])  27.7 us
  transfers between devices with their start and end apart: 39, of which 12 were waited for; matrix products, arithmetic and copies ran while one was open for 3% of the time, Pallas kernels for 29%

profile of v2, /device:TPU:0, one launch (start us, length us, event | category | flops | bytes accessed | tf_op | source)
XLA Modules:
  0.0 107.7 jit_solution(5721299687579874163)
XLA Ops:
  0.0 3.0 %collective-permute-start.3 = (bf16[576,128]{1,0:T(8,128)(2,1)}, bf16[576,128]{1,0:T(8,128)(2,1)S(1)}, u32[]{:S(2)}, u32[]{:S(2)}) collective-permute-start(bf16[576,128]{1,0:T(8,128)(2,1)} %refs_0_.1), channel_id=1, source_target_pairs={{0,16},{1,17},{2,18},{3,19},{4,20},{5,21},{6,22},{7,23},{8,24},{9,... | collective-permute-start | bytes 442376 | tf_op jit(solution)/shard_map/ppermute | solution.py:560
  3.5 4.0 %collective-permute-done.3.refs_4_ = bf16[576,128]{1,0:T(8,128)(2,1)S(1)} collective-permute-done((bf16[576,128]{1,0:T(8,128)(2,1)}, bf16[576,128]{1,0:T(8,128)(2,1)S(1)}, u32[]{:S(2)}, u32[]{:S(2)}) %collective-permute-start.3) | collective-permute-done | bytes 147488 | tf_op jit(solution)/shard_map/ppermute | solution.py:560
  11.9 3.8 %shard_map.138 = (bf16[32,2048]{1,0:T(8,128)(2,1)S(1)}, bf16[2048,1792]{1,0:T(8,128)(2,1)S(1)}) custom-call(s32[10]{0:T(128)S(1)} %pad_add_fusion.1.refs_0_, bf16[512,512]{1,0:T(8,128)(2,1)S(1)} %bitcast.47, bf16[512,64]{1,0:T(8,128)(2,1)S(1)} %bitcast.48, bf16[576,128]{1,0:T(8,128)(2,1)S(1)} %get-tuple-element.50.refs_3_, ...), custom_call_target="tpu_custom_call" | custom-call | flops 713031680 | tf_op jit(solution)/shard_map/pallas_call | solution.py:58
  17.5 3.7 %collective-permute-done.9.refs_1_ = bf16[32,2048]{1,0:T(8,128)(2,1)S(1)} collective-permute-done((bf16[32,2048]{1,0:T(8,128)(2,1)S(1)}, bf16[32,2048]{1,0:T(8,128)(2,1)S(1)}, u32[]{:S(2)}, u32[]{:S(2)}) %collective-permute-start.9) | collective-permute-done | bytes 131104 | tf_op jit(solution)/shard_map/ppermute | solution.py:560
  24.2 1.9 %shard_map.139 = (bf16[64,1792]{1,0:T(8,128)(2,1)S(1)}, f32[64,1792]{1,0:T(8,128)S(1)}) custom-call(s32[2]{0:T(128)S(1)} %pad_add_fusion.idx_ref.refs_0_, bf16[32,2048]{1,0:T(8,128)(2,1)S(1)} %get-tuple-element.53.refs_0_, bf16[32,2048]{1,0:T(8,128)(2,1)S(1)} %collective-permute-done.9.refs_1_, bf16[32,2048]{1,0:T(8,128)(2,1)S(1)} %collective-permute-done.10.refs_2_, ...), custom_call_target="tpu_custom_call" | custom-call | flops 939524096 | tf_op jit(solution)/shard_map/pallas_call | solution.py:58
  27.7 2.6 %shard_map.146 = (bf16[2,896,512]{2,1,0:T(8,128)(2,1)S(1)}, bf16[2,896,512]{2,1,0:T(8,128)(2,1)S(1)}) custom-call(s32[2]{0:T(128)S(1)} %pad_add_fusion.idx_ref.refs_0_, bf16[2,7168,512]{2,1,0:T(8,128)(2,1)} %wg_ref.9, bf16[2,7168,512]{2,1,0:T(8,128)(2,1)} %wu_ref.9), custom_call_target="tpu_custom_call" | custom-call | flops 1073741824 | tf_op jit(solution)/shard_map/pallas_call | solution.py:58
  30.4 3.7 %shard_map.144 = (bf16[2,1792,512]{2,1,0:T(8,128)(2,1)S(1)}, bf16[2,1792,512]{2,1,0:T(8,128)(2,1)S(1)}) custom-call(s32[2]{0:T(128)S(1)} %pad_add_fusion.idx_ref.refs_0_, bf16[2,7168,512]{2,1,0:T(8,128)(2,1)} %wg_ref.9, bf16[2,7168,512]{2,1,0:T(8,128)(2,1)} %wu_ref.9), custom_call_target="tpu_custom_call" | custom-call | flops 1073741824 | tf_op jit(solution)/shard_map/pallas_call | solution.py:58
  34.1 2.6 %shard_map.145 = (bf16[2,896,512]{2,1,0:T(8,128)(2,1)S(1)}, bf16[2,896,512]{2,1,0:T(8,128)(2,1)S(1)}) custom-call(s32[2]{0:T(128)S(1)} %pad_add_fusion.idx_ref.refs_0_, bf16[2,7168,512]{2,1,0:T(8,128)(2,1)} %wg_ref.9, bf16[2,7168,512]{2,1,0:T(8,128)(2,1)} %wu_ref.9), custom_call_target="tpu_custom_call" | custom-call | flops 1073741824 | tf_op jit(solution)/shard_map/pallas_call | solution.py:58
  38.5 2.6 %collective-permute-start.14 = (bf16[16,1792]{1,0:T(8,128)(2,1)S(1)}, bf16[16,1792]{1,0:T(8,128)(2,1)S(1)}, u32[]{:S(2)}, u32[]{:S(2)}) collective-permute-start(bf16[16,1792]{1,0:T(8,128)(2,1)S(1)} %get-tuple-element.103), channel_id=1, source_target_pairs={{0,4},{1,5},{2,6},{3,7},{4,0},{5,1},{6,2},{7,3},{8,12},{9,13},{10,... | collective-permute-start | bytes 172040 | tf_op jit(solution)/shard_map/ppermute | solution.py:560
  41.3 3.7 %shard_map.142 = (bf16[2,1792,512]{2,1,0:T(8,128)(2,1)S(1)}, bf16[2,1792,512]{2,1,0:T(8,128)(2,1)S(1)}) custom-call(s32[2]{0:T(128)S(1)} %pad_add_fusion.idx_ref.refs_0_, bf16[2,7168,512]{2,1,0:T(8,128)(2,1)} %wg_ref.9, bf16[2,7168,512]{2,1,0:T(8,128)(2,1)} %wu_ref.9), custom_call_target="tpu_custom_call" | custom-call | flops 1073741824 | tf_op jit(solution)/shard_map/pallas_call | solution.py:58
  45.1 1.9 %collective-permute-done.15.refs_7_ = bf16[16,1792]{1,0:T(8,128)(2,1)S(1)} collective-permute-done((bf16[16,1792]{1,0:T(8,128)(2,1)S(1)}, bf16[16,1792]{1,0:T(8,128)(2,1)S(1)}, u32[]{:S(2)}, u32[]{:S(2)}) %collective-permute-start.15) | collective-permute-done | bytes 57376 | tf_op jit(solution)/shard_map/ppermute | solution.py:560
  51.4 3.7 %shard_map.143 = (bf16[2,1792,512]{2,1,0:T(8,128)(2,1)S(1)}, bf16[2,1792,512]{2,1,0:T(8,128)(2,1)S(1)}) custom-call(s32[2]{0:T(128)S(1)} %pad_add_fusion.idx_ref.refs_0_, bf16[2,7168,512]{2,1,0:T(8,128)(2,1)} %wg_ref.9, bf16[2,7168,512]{2,1,0:T(8,128)(2,1)} %wu_ref.9), custom_call_target="tpu_custom_call" | custom-call | flops 1073741824 | tf_op jit(solution)/shard_map/pallas_call | solution.py:58
  55.5 1.8 %collective-permute-start.26 = (bf16[1,64,1024]{2,1,0:T(8,128)(2,1)S(1)}, bf16[1,64,1024]{2,1,0:T(8,128)(2,1)S(1)}, u32[]{:S(2)}, u32[]{:S(2)}) collective-permute-start(bf16[1,64,1024]{2,1,0:T(8,128)(2,1)S(1)} %get-tuple-element.96), channel_id=1, source_target_pairs={{0,16},{1,17},{2,18},{3,19},{4,20},{5,21},{6,22},{7,23},{8,24},{9,... | collective-permute-start | bytes 393224 | tf_op jit(solution)/shard_map/ppermute | solution.py:560
  57.9 2.6 %collective-permute-done.26 = bf16[1,64,1024]{2,1,0:T(8,128)(2,1)S(1)} collective-permute-done((bf16[1,64,1024]{2,1,0:T(8,128)(2,1)S(1)}, bf16[1,64,1024]{2,1,0:T(8,128)(2,1)S(1)}, u32[]{:S(2)}, u32[]{:S(2)}) %collective-permute-start.26) | collective-permute-done | bytes 131104 | tf_op jit(solution)/shard_map/ppermute | solution.py:560
  61.1 2.3 %collective-permute-done.22 = bf16[1,64,896]{2,1,0:T(8,128)(2,1)S(1)} collective-permute-done((bf16[1,64,896]{2,1,0:T(8,128)(2,1)S(1)}, bf16[1,64,896]{2,1,0:T(8,128)(2,1)S(1)}, u32[]{:S(2)}, u32[]{:S(2)}) %collective-permute-start.22) | collective-permute-done | bytes 114720 | tf_op jit(solution)/shard_map/ppermute | solution.py:560
  63.5 3.1 %shard_map.151.refs_1_ = bf16[512,7168]{1,0:T(8,128)(2,1)S(1)} custom-call(bf16[1024,7168]{1,0:T(8,128)(2,1)} %bitcast.55), custom_call_target="tpu_custom_call" | custom-call | flops 1073741824 | tf_op jit(solution)/shard_map/pallas_call | solution.py:58
  66.6 2.0 %shard_map.150.refs_0_ = bf16[256,7168]{1,0:T(8,128)(2,1)S(1)} custom-call(bf16[1024,7168]{1,0:T(8,128)(2,1)} %bitcast.56), custom_call_target="tpu_custom_call" | custom-call | flops 1073741824 | tf_op jit(solution)/shard_map/pallas_call | solution.py:58
  71.1 2.4 %shard_map.148 = (f32[2,128,512]{2,1,0:T(8,128)S(1)}, f32[2,128,512]{2,1,0:T(8,128)S(1)}, f32[128,16]{1,0:T(8,128)S(1)}, f32[128,1]{1,0:T(8,128)S(1)}) custom-call(s32[2]{0:T(128)S(1)} %pad_add_fusion.idx_ref.refs_0_, bf16[128,896]{1,0:T(8,128)(2,1)S(1)} %bitcast.52, bf16[64,1024]{1,0:T(8,128)(2,1)S(1)} %get-tuple-element.95.refs_2_, ...), custom_call_target="tpu_custom_call" | custom-call | flops 1409286144 | tf_op jit(solution)/shard_map/pallas_call | solution.py:58
  73.6 3.1 %shard_map.149 = (bf16[128,1024]{1,0:T(8,128)(2,1)S(1)}, bf16[256,7168]{1,0:T(8,128)(2,1)S(1)}) custom-call(s32[2]{0:T(128)S(1)} %pad_add_fusion.idx_ref.refs_0_, bf16[128,896]{1,0:T(8,128)(2,1)S(1)} %bitcast.50, bf16[128,896]{1,0:T(8,128)(2,1)S(1)} %bitcast.51, bf16[64,1024]{1,0:T(8,128)(2,1)S(1)} %get-tuple-element.94.refs_3_, ...), custom_call_target="tpu_custom_call" | custom-call | flops 1879048192 | tf_op jit(solution)/shard_map/pallas_call | solution.py:58
  79.4 2.0 %collective-permute-start.17 = (bf16[4,1792]{1,0:T(4,128)(2,1)S(1)}, bf16[4,1792]{1,0:T(4,128)(2,1)S(1)}, u32[]{:S(2)}, u32[]{:S(2)}) collective-permute-start(bf16[4,1792]{1,0:T(4,128)(2,1)S(1)} %get-tuple-element.60), channel_id=1, source_target_pairs={{0,16},{1,17},{2,18},{3,19},{4,20},{5,21},{6,22},{7,23},{8,24},{9,... | collective-permute-start | bytes 43016 | tf_op jit(solution)/shard_map/ppermute | solution.py:560
  84.6 1.8 %collective-permute-start.31 = (bf16[32,3584]{1,0:T(8,128)(2,1)S(1)}, bf16[32,3584]{1,0:T(8,128)(2,1)S(1)}, u32[]{:S(2)}, u32[]{:S(2)}) collective-permute-start(bf16[32,3584]{1,0:T(8,128)(2,1)S(1)} %slice.154), channel_id=1, source_target_pairs={{0,16},{1,17},{2,18},{3,19},{4,20},{5,21},{6,22},{7,23},{8,24},{9,... | collective-permute-start | bytes 688136 | tf_op jit(solution)/shard_map/ppermute | solution.py:560
  86.4 4.4 %collective-permute-done.34 = bf16[32,3584]{1,0:T(8,128)(2,1)S(1)} collective-permute-done((bf16[32,3584]{1,0:T(8,128)(2,1)S(1)}, bf16[32,3584]{1,0:T(8,128)(2,1)S(1)}, u32[]{:S(2)}, u32[]{:S(2)}) %collective-permute-start.34) | collective-permute-done | bytes 229408 | tf_op jit(solution)/shard_map/ppermute | solution.py:560
  93.6 2.1 %collective-permute-done.35 = bf16[16,3584]{1,0:T(8,128)(2,1)S(1)} collective-permute-done((bf16[16,3584]{1,0:T(8,128)(2,1)S(1)}, bf16[16,3584]{1,0:T(8,128)(2,1)S(1)}, u32[]{:S(2)}, u32[]{:S(2)}) %collective-permute-start.35) | collective-permute-done | bytes 114720 | tf_op jit(solution)/shard_map/ppermute | solution.py:560
  102.2 2.5 %collective-permute-done.37.refs_6_ = bf16[4,7168]{1,0:T(4,128)(2,1)S(1)} collective-permute-done((bf16[4,7168]{1,0:T(4,128)(2,1)S(1)}, bf16[4,7168]{1,0:T(4,128)(2,1)S(1)}, u32[]{:S(2)}, u32[]{:S(2)}) %collective-permute-start.37) | collective-permute-done | bytes 57376 | tf_op jit(solution)/shard_map/ppermute | solution.py:560
  (113 shorter events, 39.6 us)
Async XLA Ops:
  0.0 7.5 %collective-permute-start.3 = (bf16[576,128]{1,0:T(8,128)(2,1)}, bf16[576,128]{1,0:T(8,128)(2,1)S(1)}, u32[]{:S(2)}, u32[]{:S(2)}) collective-permute-start(bf16[576,128]{1,0:T(8,128)(2,1)} %refs_0_.1), channel_id=1, source_target_pairs={{0,16},{1,17},{2,18},{3,19},{4,20},{5,21},{6,22},{7,23},{8,24},{9,... | collective-permute-start | bytes 442376 | tf_op jit(solution)/shard_map/ppermute | solution.py:560
  3.0 8.8 %collective-permute-start.7 = (bf16[32,576]{1,0:T(8,128)(2,1)}, bf16[32,576]{1,0:T(8,128)(2,1)S(1)}, u32[]{:S(2)}, u32[]{:S(2)}) collective-permute-start(bf16[32,576]{1,0:T(8,128)(2,1)} %bitcast.66), channel_id=1, source_target_pairs={{0,8},{1,9},{2,10},{3,11},{4,12},{5,13},{6,14},{7,15},{8,0},{9,1},... | collective-permute-start | bytes 110600 | tf_op jit(solution)/shard_map/ppermute | solution.py:560
  3.0 8.8 %collective-permute-start.4 = (bf16[576,128]{1,0:T(8,128)(2,1)}, bf16[576,128]{1,0:T(8,128)(2,1)S(1)}, u32[]{:S(2)}, u32[]{:S(2)}) collective-permute-start(bf16[576,128]{1,0:T(8,128)(2,1)} %refs_0_.1), channel_id=1, source_target_pairs={{0,8},{1,9},{2,10},{3,11},{4,12},{5,13},{6,14},{7,15},{8,0},{9,1},... | collective-permute-start | bytes 442376 | tf_op jit(solution)/shard_map/ppermute | solution.py:560
  15.7 5.5 %collective-permute-start.9 = (bf16[32,2048]{1,0:T(8,128)(2,1)S(1)}, bf16[32,2048]{1,0:T(8,128)(2,1)S(1)}, u32[]{:S(2)}, u32[]{:S(2)}) collective-permute-start(bf16[32,2048]{1,0:T(8,128)(2,1)S(1)} %get-tuple-element.53.refs_0_), channel_id=1, source_target_pairs={{0,16},{1,17},{2,18},{3,19},{4,20},{5,21},{6,22},{7,23},{8,24},{9,... | collective-permute-start | bytes 393224 | tf_op jit(solution)/shard_map/ppermute | solution.py:560
  17.5 6.7 %collective-permute-start.10 = (bf16[32,2048]{1,0:T(8,128)(2,1)S(1)}, bf16[32,2048]{1,0:T(8,128)(2,1)S(1)}, u32[]{:S(2)}, u32[]{:S(2)}) collective-permute-start(bf16[32,2048]{1,0:T(8,128)(2,1)S(1)} %get-tuple-element.53.refs_0_), channel_id=1, source_target_pairs={{0,8},{1,9},{2,10},{3,11},{4,12},{5,13},{6,14},{7,15},{8,0},{9,1},... | collective-permute-start | bytes 393224 | tf_op jit(solution)/shard_map/ppermute | solution.py:560
  21.9 19.2 %collective-permute-start = (bf16[4,1920]{1,0:T(4,128)(2,1)S(1)}, bf16[4,1920]{1,0:T(4,128)(2,1)S(1)}, u32[]{:S(2)}, u32[]{:S(2)}) collective-permute-start(bf16[4,1920]{1,0:T(4,128)(2,1)S(1)} %get-tuple-element.47), channel_id=1, source_target_pairs={{0,8},{1,9},{2,10},{3,11},{4,12},{5,13},{6,14},{7,15},{8,0},{9,1},... | collective-permute-start | bytes 46088 | tf_op jit(solution)/shard_map/ppermute | solution.py:560
  22.5 22.6 %collective-permute-start.1 = (bf16[4,1920]{1,0:T(4,128)(2,1)S(1)}, bf16[4,1920]{1,0:T(4,128)(2,1)S(1)}, u32[]{:S(2)}, u32[]{:S(2)}) collective-permute-start(bf16[4,1920]{1,0:T(4,128)(2,1)S(1)} %get-tuple-element.48), channel_id=1, source_target_pairs={{0,16},{1,17},{2,18},{3,19},{4,20},{5,21},{6,22},{7,23},{8,24},{9,... | collective-permute-start | bytes 46088 | tf_op jit(solution)/shard_map/ppermute | solution.py:560
  24.2 20.9 %collective-permute-start.2 = (bf16[4,1920]{1,0:T(4,128)(2,1)S(1)}, bf16[4,1920]{1,0:T(4,128)(2,1)S(1)}, u32[]{:S(2)}, u32[]{:S(2)}) collective-permute-start(bf16[4,1920]{1,0:T(4,128)(2,1)S(1)} %get-tuple-element.49), channel_id=1, source_target_pairs={{0,24},{1,25},{2,26},{3,27},{4,28},{5,29},{6,30},{7,31},{8,16},{9,... | collective-permute-start | bytes 46088 | tf_op jit(solution)/shard_map/ppermute | solution.py:560
  26.2 10.6 %collective-permute-start.12 = (bf16[64,1792]{1,0:T(8,128)(2,1)S(1)}, bf16[64,1792]{1,0:T(8,128)(2,1)S(1)}, u32[]{:S(2)}, u32[]{:S(2)}) collective-permute-start(bf16[64,1792]{1,0:T(8,128)(2,1)S(1)} %get-tuple-element.56), channel_id=1, source_target_pairs={{0,1},{1,0},{2,3},{3,2},{4,5},{5,4},{6,7},{7,6},{8,9},{9,8},{10,11... | collective-permute-start | bytes 688136 | tf_op jit(solution)/shard_map/ppermute | solution.py:560
  36.8 8.3 %collective-permute-start.13 = (bf16[16,1792]{1,0:T(8,128)(2,1)S(1)}, bf16[16,1792]{1,0:T(8,128)(2,1)S(1)}, u32[]{:S(2)}, u32[]{:S(2)}) collective-permute-start(bf16[16,1792]{1,0:T(8,128)(2,1)S(1)} %get-tuple-element.104), channel_id=1, source_target_pairs={{0,2},{1,3},{2,0},{3,1},{4,6},{5,7},{6,4},{7,5},{8,10},{9,11},{10,... | collective-permute-start | bytes 172040 | tf_op jit(solution)/shard_map/ppermute | solution.py:560
  38.5 6.6 %collective-permute-start.14 = (bf16[16,1792]{1,0:T(8,128)(2,1)S(1)}, bf16[16,1792]{1,0:T(8,128)(2,1)S(1)}, u32[]{:S(2)}, u32[]{:S(2)}) collective-permute-start(bf16[16,1792]{1,0:T(8,128)(2,1)S(1)} %get-tuple-element.103), channel_id=1, source_target_pairs={{0,4},{1,5},{2,6},{3,7},{4,0},{5,1},{6,2},{7,3},{8,12},{9,13},{10,... | collective-permute-start | bytes 172040 | tf_op jit(solution)/shard_map/ppermute | solution.py:560
  41.1 6.0 %collective-permute-start.15 = (bf16[16,1792]{1,0:T(8,128)(2,1)S(1)}, bf16[16,1792]{1,0:T(8,128)(2,1)S(1)}, u32[]{:S(2)}, u32[]{:S(2)}) collective-permute-start(bf16[16,1792]{1,0:T(8,128)(2,1)S(1)} %get-tuple-element.102), channel_id=1, source_target_pairs={{0,6},{1,7},{2,4},{3,5},{4,2},{5,3},{6,0},{7,1},{8,14},{9,15},{10,... | collective-permute-start | bytes 172040 | tf_op jit(solution)/shard_map/ppermute | solution.py:560
  47.9 7.2 %collective-permute-start.20 = (bf16[16,1920]{1,0:T(8,128)(2,1)S(1)}, bf16[16,1920]{1,0:T(8,128)(2,1)S(1)}, u32[]{:S(2)}, u32[]{:S(2)}) collective-permute-start(bf16[16,1920]{1,0:T(8,128)(2,1)S(1)} %get-tuple-element.62), channel_id=1, source_target_pairs={{0,4},{1,5},{2,6},{3,7},{4,0},{5,1},{6,2},{7,3},{8,12},{9,13},{10,... | collective-permute-start | bytes 184328 | tf_op jit(solution)/shard_map/ppermute | solution.py:560
  49.4 6.0 %collective-permute-start.21 = (bf16[16,1920]{1,0:T(8,128)(2,1)S(1)}, bf16[16,1920]{1,0:T(8,128)(2,1)S(1)}, u32[]{:S(2)}, u32[]{:S(2)}) collective-permute-start(bf16[16,1920]{1,0:T(8,128)(2,1)S(1)} %get-tuple-element.62), channel_id=1, source_target_pairs={{0,6},{1,7},{2,4},{3,5},{4,2},{5,3},{6,0},{7,1},{8,14},{9,15},{10,... | collective-permute-start | bytes 184328 | tf_op jit(solution)/shard_map/ppermute | solution.py:560
  57.3 6.1 %collective-permute-start.22 = (bf16[1,64,896]{2,1,0:T(8,128)(2,1)S(1)}, bf16[1,64,896]{2,1,0:T(8,128)(2,1)S(1)}, u32[]{:S(2)}, u32[]{:S(2)}) collective-permute-start(bf16[1,64,896]{2,1,0:T(8,128)(2,1)S(1)} %slice_bitcast_fusion.6), channel_id=1, source_target_pairs={{0,1},{1,0},{2,3},{3,2},{4,5},{5,4},{6,7},{7,6},{8,9},{9,8},{10,11... | collective-permute-start | bytes 344072 | tf_op jit(solution)/shard_map/ppermute | solution.py:560
  60.5 10.2 %collective-permute-start.28 = (bf16[2,64,1024]{2,1,0:T(8,128)(2,1)S(1)}, bf16[2,64,1024]{2,1,0:T(8,128)(2,1)S(1)}, u32[]{:S(2)}, u32[]{:S(2)}) collective-permute-start(bf16[2,64,1024]{2,1,0:T(8,128)(2,1)S(1)} %pad_maximum_fusion.1), channel_id=1, source_target_pairs={{0,1},{1,0},{2,3},{3,2},{4,5},{5,4},{6,7},{7,6},{8,9},{9,8},{10,11... | collective-permute-start | bytes 786440 | tf_op jit(solution)/shard_map/ppermute | solution.py:560
  63.4 7.2 %collective-permute-start.24 = (bf16[1,128,896]{2,1,0:T(8,128)(2,1)S(1)}, bf16[1,128,896]{2,1,0:T(8,128)(2,1)S(1)}, u32[]{:S(2)}, u32[]{:S(2)}) collective-permute-start(bf16[1,128,896]{2,1,0:T(8,128)(2,1)S(1)} %get-tuple-element.101), channel_id=1, source_target_pairs={{0,16},{1,17},{2,18},{3,19},{4,20},{5,21},{6,22},{7,23},{8,24},{9,... | collective-permute-start | bytes 688136 | tf_op jit(solution)/shard_map/ppermute | solution.py:560
  79.0 21.5 %collective-permute-start.16 = (bf16[4,1792]{1,0:T(4,128)(2,1)S(1)}, bf16[4,1792]{1,0:T(4,128)(2,1)S(1)}, u32[]{:S(2)}, u32[]{:S(2)}) collective-permute-start(bf16[4,1792]{1,0:T(4,128)(2,1)S(1)} %get-tuple-element.59), channel_id=1, source_target_pairs={{0,8},{1,9},{2,10},{3,11},{4,12},{5,13},{6,14},{7,15},{8,0},{9,1},... | collective-permute-start | bytes 43016 | tf_op jit(solution)/shard_map/ppermute | solution.py:560
  79.4 22.8 %collective-permute-start.17 = (bf16[4,1792]{1,0:T(4,128)(2,1)S(1)}, bf16[4,1792]{1,0:T(4,128)(2,1)S(1)}, u32[]{:S(2)}, u32[]{:S(2)}) collective-permute-start(bf16[4,1792]{1,0:T(4,128)(2,1)S(1)} %get-tuple-element.60), channel_id=1, source_target_pairs={{0,16},{1,17},{2,18},{3,19},{4,20},{5,21},{6,22},{7,23},{8,24},{9,... | collective-permute-start | bytes 43016 | tf_op jit(solution)/shard_map/ppermute | solution.py:560
  81.4 20.8 %collective-permute-start.18 = (bf16[4,1792]{1,0:T(4,128)(2,1)S(1)}, bf16[4,1792]{1,0:T(4,128)(2,1)S(1)}, u32[]{:S(2)}, u32[]{:S(2)}) collective-permute-start(bf16[4,1792]{1,0:T(4,128)(2,1)S(1)} %get-tuple-element.61), channel_id=1, source_target_pairs={{0,24},{1,25},{2,26},{3,27},{4,28},{5,29},{6,30},{7,31},{8,16},{9,... | collective-permute-start | bytes 43016 | tf_op jit(solution)/shard_map/ppermute | solution.py:560
  82.9 7.9 %collective-permute-start.34 = (bf16[32,3584]{1,0:T(8,128)(2,1)S(1)}, bf16[32,3584]{1,0:T(8,128)(2,1)S(1)}, u32[]{:S(2)}, u32[]{:S(2)}) collective-permute-start(bf16[32,3584]{1,0:T(8,128)(2,1)S(1)} %slice.153), channel_id=1, source_target_pairs={{0,1},{1,0},{2,3},{3,2},{4,5},{5,4},{6,7},{7,6},{8,9},{9,8},{10,11... | collective-permute-start | bytes 688136 | tf_op jit(solution)/shard_map/ppermute | solution.py:560
  84.6 8.1 %collective-permute-start.31 = (bf16[32,3584]{1,0:T(8,128)(2,1)S(1)}, bf16[32,3584]{1,0:T(8,128)(2,1)S(1)}, u32[]{:S(2)}, u32[]{:S(2)}) collective-permute-start(bf16[32,3584]{1,0:T(8,128)(2,1)S(1)} %slice.154), channel_id=1, source_target_pairs={{0,16},{1,17},{2,18},{3,19},{4,20},{5,21},{6,22},{7,23},{8,24},{9,... | collective-permute-start | bytes 688136 | tf_op jit(solution)/shard_map/ppermute | solution.py:560
  98.7 6.0 %collective-permute-start.37 = (bf16[4,7168]{1,0:T(4,128)(2,1)S(1)}, bf16[4,7168]{1,0:T(4,128)(2,1)S(1)}, u32[]{:S(2)}, u32[]{:S(2)}) collective-permute-start(bf16[4,7168]{1,0:T(4,128)(2,1)S(1)} %get-tuple-element.98), channel_id=1, source_target_pairs={{0,4},{1,5},{2,6},{3,7},{4,0},{5,1},{6,2},{7,3},{8,12},{9,13},{10,... | collective-permute-start | bytes 172040 | tf_op jit(solution)/shard_map/ppermute | solution.py:560
  100.5 6.0 %collective-permute-start.38 = (bf16[4,7168]{1,0:T(4,128)(2,1)S(1)}, bf16[4,7168]{1,0:T(4,128)(2,1)S(1)}, u32[]{:S(2)}, u32[]{:S(2)}) collective-permute-start(bf16[4,7168]{1,0:T(4,128)(2,1)S(1)} %get-tuple-element.97), channel_id=1, source_target_pairs={{0,6},{1,7},{2,4},{3,5},{4,2},{5,3},{6,0},{7,1},{8,14},{9,15},{10,... | collective-permute-start | bytes 172040 | tf_op jit(solution)/shard_map/ppermute | solution.py:560
  (20 other events, 97.4 us)

commit v3 on v2

--- a/solution.py
+++ b/solution.py
@@ -238,47 +238,61 @@
     return ((r == q + shift * tok)).astype(F32).astype(BF)
 
 
-def merge(idx, parts, own, got, gain, tok):
+def place_rows(idx, parts, gain, blk, tok):
     nctx = len(parts)
+    wide = parts[0].shape[1]
+    cols = wide - EXTRA
+
+    def kernel(idx_ref, *refs):
+        c = idx_ref[0]
+        gain_ref, res_ref, row_ref = refs[nctx:]
+        res = None
+        for k in range(nctx):
+            part = dot(one_hot_rows(blk, tok, tok, c ^ k), refs[k][...])
+            res = part if res is None else res + part
+        res_ref[...] = res
+        row_ref[...] = choose(
+            [(c == j, gain_ref[:, j * cols : (j + 1) * cols]) for j in range(nctx)]
+        )
+
+    return call(
+        kernel,
+        [((blk, wide), F32), ((1, cols), F32)],
+        (idx, *parts, gain),
+        (pltpu.SMEM,) + (pltpu.VMEM,) * (nctx + 1),
+        4,
+        1 << 28,
+    )
+
+
+def merge(res, gain, own, got):
     blk, cols = own.shape
     n = len(got)
 
-    def kernel(idx_ref, *refs):
-        c = idx_ref[0]
-        prefs = refs[:nctx]
-        own_ref = refs[nctx]
-        grefs = refs[nctx + 1 : nctx + 1 + n]
-        gain_ref, sx_ref, att_ref = refs[nctx + 1 + n :]
+    def kernel(res_ref, gain_ref, own_ref, *refs):
+        sx_ref, att_ref = refs[n:]
         att = own_ref[...]
-        for g in grefs:
+        for g in refs[:n]:
             att = att + g[...].astype(F32)
         att = att.astype(BF)
         att_ref[...] = att
-        res = None
-        for k in range(nctx):
-            part = dot(one_hot_rows(blk, tok, tok, c ^ k), prefs[k][...])
-            res = part if res is None else res + part
-        hidden = res[:, :cols] + att.astype(F32)
+        hidden = res_ref[:, :cols] + att.astype(F32)
         ssq = jnp.sum(hidden * hidden, axis=1, keepdims=True)
-        gain = choose(
-            [(c == j, gain_ref[:, j * cols : (j + 1) * cols]) for j in range(nctx)]
-        )
-        scaled = hidden * gain
         hi = ssq.astype(BF).astype(F32)
         mid = (ssq - hi).astype(BF).astype(F32)
         low = ssq - hi - mid
-        extra = res[:, cols:]
+        extra = res_ref[:, cols:]
         lane = lax.broadcasted_iota(I32, extra.shape, 1)
         extra = jnp.where(lane == 0, hi, jnp.where(lane == 1, mid, extra))
         extra = jnp.where(lane == 2, low, extra)
-        sx_ref[:, :cols] = scaled.astype(BF)
+        sx_ref[:, :cols] = (hidden * gain_ref[...]).astype(BF)
         sx_ref[:, cols:] = extra.astype(BF)
 
     return call(
         kernel,
         [((blk, cols + EXTRA), BF), ((blk, cols), BF)],
-        (idx, *parts, own, *got, gain),
-        (pltpu.SMEM,) + (pltpu.VMEM,) * (nctx + n + 2),
+        (res, gain, own, *got),
+        (pltpu.VMEM,) * (n + 3),
         4,
         1 << 28,
     )
@@ -456,6 +470,8 @@
                     outs[c_i][e] = product(e, c_i)
             outs[2][...] = logit
             outs[3][...] = ssum
+            if copy:
+                load.wait()
             return
         scale = lax.rsqrt(ssum / width + NORM_EPS)
         affinity = jax.nn.sigmoid(logit * scale) * chosen
@@ -605,7 +621,6 @@
     w_down = w_down.reshape(-1, width)
     dq = w_down.shape[0] // 4
     down_v = grab((w_down,), 0, dq)
-    down_v += grab((w_down,), dq, 2 * dq)
 
     res_got = residual_parts(idx, residual, expert_ids, nctx)
     res_got = [swap(p, cm=k) if k else p for k, p in enumerate(res_got)]
@@ -620,7 +635,8 @@
         for i, m in enumerate(zsub)
         if m
     ]
-    sx, att_blk = merge(idx, res_got, summed[:blk], got, norm_gain[None], tok)
+    res_rows, gain_row = place_rows(idx, res_got, norm_gain[None], blk, tok)
+    sx, att_blk = merge(res_rows, gain_row, summed[:blk], got)
 
     zx = jnp.stack([swap(sx, em=m) if m else sx for m in zsub])
     zx = zx.reshape(len(zsub) * blk, -1)
@@ -642,7 +658,10 @@
 
     router = router_weight.reshape(2 * nctx, hc, nexperts).transpose(0, 2, 1)
     first = [Chunk([own_a[0]], 0, 0)]
-    g1 = experts(idx, first, router, groups_1, width, (), None)
+    *g1, down_1 = experts(
+        idx, first, router, groups_1, width, (), None, (w_down, dq, 2 * dq)
+    )
+    down_v.append(down_1)
     second = [Chunk([rest_a[i - 1]], xorder[i], 0) for i in range(1, nx)]
     second += [Chunk([xb[i], far_b[i]], xorder[i], 1) for i in range(nx)]
     g2 = experts(idx, second, router, groups_2, width, g1, None)

time: 108 us -> 109 us (level)
  waiting for transfers between devices: 27.7 us -> 29.3 us
    ppermute x39, waiting for transfers between devices: 27.7 us -> 29.3 us  [swap(): lax.ppermute(x, ('ctx', 'exp'), [(i, i ^ m) for i in range(nctx * nexp)])]
  transfers between devices with their start and end apart: 39 -> 39, of which waited for: 12 -> 15; matrix products, arithmetic and copies ran while one was open for 3% -> 3% of each run, Pallas kernels for 29% -> 27%
where the time goes in v3:
time: 109 us; the launch traced here: 108 us
  Pallas kernels  40.8 us (37%)
  starting transfers between devices  34.6 us (32%)
  waiting for transfers between devices  29.3 us (27%)
  local copies, waits for them, and re-layouts  1.63 us (1%)
  other arithmetic  1.35 us (1%)
    pallas_call x19, Pallas kernels, call(): pl.pallas_call(kernel, out_shape=tuple(shapes), in_specs=[pl.BlockSpec(me...  40.8 us
    ppermute x39, starting transfers between devices, swap(): lax.ppermute(x, ('ctx', 'exp'), [(i, i ^ m) for i in range(nctx * nexp)])  34.6 us
    ppermute x39, waiting for transfers between devices, swap(): lax.ppermute(x, ('ctx', 'exp'), [(i, i ^ m) for i in range(nctx * nexp)])  29.3 us
  transfers between devices with their start and end apart: 39, of which 15 were waited for; matrix products, arithmetic and copies ran while one was open for 3% of the time, Pallas kernels for 27%

profile of v3, /device:TPU:0, one launch (start us, length us, event | category | flops | bytes accessed | tf_op | source)
XLA Modules:
  0.0 108.2 jit_solution(8988869236472258292)
XLA Ops:
  0.0 3.0 %collective-permute-start.3 = (bf16[576,128]{1,0:T(8,128)(2,1)}, bf16[576,128]{1,0:T(8,128)(2,1)S(1)}, u32[]{:S(2)}, u32[]{:S(2)}) collective-permute-start(bf16[576,128]{1,0:T(8,128)(2,1)} %refs_0_.1), channel_id=1, source_target_pairs={{0,16},{1,17},{2,18},{3,19},{4,20},{5,21},{6,22},{7,23},{8,24},{9,... | collective-permute-start | bytes 442376 | tf_op jit(solution)/shard_map/ppermute | solution.py:576
  3.5 4.0 %collective-permute-done.3.refs_4_ = bf16[576,128]{1,0:T(8,128)(2,1)S(1)} collective-permute-done((bf16[576,128]{1,0:T(8,128)(2,1)}, bf16[576,128]{1,0:T(8,128)(2,1)S(1)}, u32[]{:S(2)}, u32[]{:S(2)}) %collective-permute-start.3) | collective-permute-done | bytes 147488 | tf_op jit(solution)/shard_map/ppermute | solution.py:576
  11.8 3.8 %shard_map.139 = (bf16[32,2048]{1,0:T(8,128)(2,1)S(1)}, bf16[2048,1792]{1,0:T(8,128)(2,1)S(1)}) custom-call(s32[10]{0:T(128)S(1)} %pad_add_fusion.1.refs_0_, bf16[512,512]{1,0:T(8,128)(2,1)S(1)} %bitcast.47, bf16[512,64]{1,0:T(8,128)(2,1)S(1)} %bitcast.48, bf16[576,128]{1,0:T(8,128)(2,1)S(1)} %get-tuple-element.55.refs_3_, ...), custom_call_target="tpu_custom_call" | custom-call | flops 713031680 | tf_op jit(solution)/shard_map/pallas_call | solution.py:58
  17.5 3.7 %collective-permute-done.9.refs_1_ = bf16[32,2048]{1,0:T(8,128)(2,1)S(1)} collective-permute-done((bf16[32,2048]{1,0:T(8,128)(2,1)S(1)}, bf16[32,2048]{1,0:T(8,128)(2,1)S(1)}, u32[]{:S(2)}, u32[]{:S(2)}) %collective-permute-start.9) | collective-permute-done | bytes 131104 | tf_op jit(solution)/shard_map/ppermute | solution.py:576
  22.5 2.0 %shard_map.140 = (bf16[64,1792]{1,0:T(8,128)(2,1)S(1)}, f32[64,1792]{1,0:T(8,128)S(1)}) custom-call(s32[2]{0:T(128)S(1)} %pad_add_fusion.idx_ref.refs_0_, bf16[32,2048]{1,0:T(8,128)(2,1)S(1)} %get-tuple-element.58.refs_0_, bf16[32,2048]{1,0:T(8,128)(2,1)S(1)} %collective-permute-done.9.refs_1_, bf16[32,2048]{1,0:T(8,128)(2,1)S(1)} %collective-permute-done.10.refs_2_, ...), custom_call_target="tpu_custom_call" | custom-call | flops 939524096 | tf_op jit(solution)/shard_map/pallas_call | solution.py:58
  24.5 1.8 %collective-permute-start.12 = (bf16[64,1792]{1,0:T(8,128)(2,1)S(1)}, bf16[64,1792]{1,0:T(8,128)(2,1)S(1)}, u32[]{:S(2)}, u32[]{:S(2)}) collective-permute-start(bf16[64,1792]{1,0:T(8,128)(2,1)S(1)} %get-tuple-element.61), channel_id=1, source_target_pairs={{0,1},{1,0},{2,3},{3,2},{4,5},{5,4},{6,7},{7,6},{8,9},{9,8},{10,11... | collective-permute-start | bytes 688136 | tf_op jit(solution)/shard_map/ppermute | solution.py:576
  28.9 2.6 %shard_map.147 = (bf16[2,896,512]{2,1,0:T(8,128)(2,1)S(1)}, bf16[2,896,512]{2,1,0:T(8,128)(2,1)S(1)}) custom-call(s32[2]{0:T(128)S(1)} %pad_add_fusion.idx_ref.refs_0_, bf16[2,7168,512]{2,1,0:T(8,128)(2,1)} %wg_ref.9, bf16[2,7168,512]{2,1,0:T(8,128)(2,1)} %wu_ref.9), custom_call_target="tpu_custom_call" | custom-call | flops 1073741824 | tf_op jit(solution)/shard_map/pallas_call | solution.py:58
  31.5 3.7 %shard_map.145 = (bf16[2,1792,512]{2,1,0:T(8,128)(2,1)S(1)}, bf16[2,1792,512]{2,1,0:T(8,128)(2,1)S(1)}) custom-call(s32[2]{0:T(128)S(1)} %pad_add_fusion.idx_ref.refs_0_, bf16[2,7168,512]{2,1,0:T(8,128)(2,1)} %wg_ref.9, bf16[2,7168,512]{2,1,0:T(8,128)(2,1)} %wu_ref.9), custom_call_target="tpu_custom_call" | custom-call | flops 1073741824 | tf_op jit(solution)/shard_map/pallas_call | solution.py:58
  37.0 2.6 %collective-permute-start.14 = (bf16[16,1792]{1,0:T(8,128)(2,1)S(1)}, bf16[16,1792]{1,0:T(8,128)(2,1)S(1)}, u32[]{:S(2)}, u32[]{:S(2)}) collective-permute-start(bf16[16,1792]{1,0:T(8,128)(2,1)S(1)} %get-tuple-element.109), channel_id=1, source_target_pairs={{0,4},{1,5},{2,6},{3,7},{4,0},{5,1},{6,2},{7,3},{8,12},{9,13},{10,... | collective-permute-start | bytes 172040 | tf_op jit(solution)/shard_map/ppermute | solution.py:576
  39.8 2.6 %shard_map.146 = (bf16[2,896,512]{2,1,0:T(8,128)(2,1)S(1)}, bf16[2,896,512]{2,1,0:T(8,128)(2,1)S(1)}) custom-call(s32[2]{0:T(128)S(1)} %pad_add_fusion.idx_ref.refs_0_, bf16[2,7168,512]{2,1,0:T(8,128)(2,1)} %wg_ref.9, bf16[2,7168,512]{2,1,0:T(8,128)(2,1)} %wu_ref.9), custom_call_target="tpu_custom_call" | custom-call | flops 1073741824 | tf_op jit(solution)/shard_map/pallas_call | solution.py:58
  43.5 2.1 %collective-permute-done.15.refs_2_ = bf16[16,1792]{1,0:T(8,128)(2,1)S(1)} collective-permute-done((bf16[16,1792]{1,0:T(8,128)(2,1)S(1)}, bf16[16,1792]{1,0:T(8,128)(2,1)S(1)}, u32[]{:S(2)}, u32[]{:S(2)}) %collective-permute-start.15) | collective-permute-done | bytes 57376 | tf_op jit(solution)/shard_map/ppermute | solution.py:576
  49.2 3.7 %shard_map.143 = (bf16[2,1792,512]{2,1,0:T(8,128)(2,1)S(1)}, bf16[2,1792,512]{2,1,0:T(8,128)(2,1)S(1)}) custom-call(s32[2]{0:T(128)S(1)} %pad_add_fusion.idx_ref.refs_0_, bf16[2,7168,512]{2,1,0:T(8,128)(2,1)} %wg_ref.9, bf16[2,7168,512]{2,1,0:T(8,128)(2,1)} %wu_ref.9), custom_call_target="tpu_custom_call" | custom-call | flops 1073741824 | tf_op jit(solution)/shard_map/pallas_call | solution.py:58
  55.4 2.9 %collective-permute-done.26 = bf16[1,64,1024]{2,1,0:T(8,128)(2,1)S(1)} collective-permute-done((bf16[1,64,1024]{2,1,0:T(8,128)(2,1)S(1)}, bf16[1,64,1024]{2,1,0:T(8,128)(2,1)S(1)}, u32[]{:S(2)}, u32[]{:S(2)}) %collective-permute-start.26) | collective-permute-done | bytes 131104 | tf_op jit(solution)/shard_map/ppermute | solution.py:576
  58.9 2.0 %collective-permute-done.22 = bf16[1,64,896]{2,1,0:T(8,128)(2,1)S(1)} collective-permute-done((bf16[1,64,896]{2,1,0:T(8,128)(2,1)S(1)}, bf16[1,64,896]{2,1,0:T(8,128)(2,1)S(1)}, u32[]{:S(2)}, u32[]{:S(2)}) %collective-permute-start.22) | collective-permute-done | bytes 114720 | tf_op jit(solution)/shard_map/ppermute | solution.py:576
  61.6 3.7 %shard_map.144 = (bf16[2,1792,512]{2,1,0:T(8,128)(2,1)S(1)}, bf16[2,1792,512]{2,1,0:T(8,128)(2,1)S(1)}) custom-call(s32[2]{0:T(128)S(1)} %pad_add_fusion.idx_ref.refs_0_, bf16[2,7168,512]{2,1,0:T(8,128)(2,1)} %wg_ref.9, bf16[2,7168,512]{2,1,0:T(8,128)(2,1)} %wu_ref.9), custom_call_target="tpu_custom_call" | custom-call | flops 1073741824 | tf_op jit(solution)/shard_map/pallas_call | solution.py:58
  65.3 2.0 %shard_map.151.refs_0_ = bf16[256,7168]{1,0:T(8,128)(2,1)S(1)} custom-call(bf16[1024,7168]{1,0:T(8,128)(2,1)} %bitcast.55), custom_call_target="tpu_custom_call" | custom-call | flops 1073741824 | tf_op jit(solution)/shard_map/pallas_call | solution.py:58
  67.4 3.6 %shard_map.148 = (f32[2,128,512]{2,1,0:T(8,128)S(1)}, f32[2,128,512]{2,1,0:T(8,128)S(1)}, f32[128,16]{1,0:T(8,128)S(1)}, f32[128,1]{1,0:T(8,128)S(1)}, bf16[512,7168]{1,0:T(8,128)(2,1)S(1)}) custom-call(s32[2]{0:T(128)S(1)} %pad_add_fusion.idx_ref.refs_0_, bf16[128,896]{1,0:T(8,128)(2,1)S(1)} %get-tuple-element.106.refs_1_, ...), custom_call_target="tpu_custom_call" | custom-call | flops 469762048 | tf_op jit(solution)/shard_map/pallas_call | solution.py:58
  72.2 2.4 %shard_map.149 = (f32[2,128,512]{2,1,0:T(8,128)S(1)}, f32[2,128,512]{2,1,0:T(8,128)S(1)}, f32[128,16]{1,0:T(8,128)S(1)}, f32[128,1]{1,0:T(8,128)S(1)}) custom-call(s32[2]{0:T(128)S(1)} %pad_add_fusion.idx_ref.refs_0_, bf16[128,896]{1,0:T(8,128)(2,1)S(1)} %bitcast.52, bf16[64,1024]{1,0:T(8,128)(2,1)S(1)} %get-tuple-element.101.refs_2_, ...), custom_call_target="tpu_custom_call" | custom-call | flops 1409286144 | tf_op jit(solution)/shard_map/pallas_call | solution.py:58
  74.7 3.1 %shard_map.150 = (bf16[128,1024]{1,0:T(8,128)(2,1)S(1)}, bf16[256,7168]{1,0:T(8,128)(2,1)S(1)}) custom-call(s32[2]{0:T(128)S(1)} %pad_add_fusion.idx_ref.refs_0_, bf16[128,896]{1,0:T(8,128)(2,1)S(1)} %bitcast.50, bf16[128,896]{1,0:T(8,128)(2,1)S(1)} %bitcast.51, bf16[64,1024]{1,0:T(8,128)(2,1)S(1)} %get-tuple-element.100.refs_3_, ...), custom_call_target="tpu_custom_call" | custom-call | flops 1879048192 | tf_op jit(solution)/shard_map/pallas_call | solution.py:58
  87.0 4.6 %collective-permute-done.34 = bf16[32,3584]{1,0:T(8,128)(2,1)S(1)} collective-permute-done((bf16[32,3584]{1,0:T(8,128)(2,1)S(1)}, bf16[32,3584]{1,0:T(8,128)(2,1)S(1)}, u32[]{:S(2)}, u32[]{:S(2)}) %collective-permute-start.34) | collective-permute-done | bytes 229408 | tf_op jit(solution)/shard_map/ppermute | solution.py:576
  94.4 2.1 %collective-permute-done.35 = bf16[16,3584]{1,0:T(8,128)(2,1)S(1)} collective-permute-done((bf16[16,3584]{1,0:T(8,128)(2,1)S(1)}, bf16[16,3584]{1,0:T(8,128)(2,1)S(1)}, u32[]{:S(2)}, u32[]{:S(2)}) %collective-permute-start.35) | collective-permute-done | bytes 114720 | tf_op jit(solution)/shard_map/ppermute | solution.py:576
  98.7 2.3 %collective-permute-start.37 = (bf16[4,7168]{1,0:T(4,128)(2,1)S(1)}, bf16[4,7168]{1,0:T(4,128)(2,1)S(1)}, u32[]{:S(2)}, u32[]{:S(2)}) collective-permute-start(bf16[4,7168]{1,0:T(4,128)(2,1)S(1)} %get-tuple-element.104), channel_id=1, source_target_pairs={{0,4},{1,5},{2,6},{3,7},{4,0},{5,1},{6,2},{7,3},{8,12},{9,13},{10,... | collective-permute-start | bytes 172040 | tf_op jit(solution)/shard_map/ppermute | solution.py:576
  101.0 1.9 %collective-permute-start.38 = (bf16[4,7168]{1,0:T(4,128)(2,1)S(1)}, bf16[4,7168]{1,0:T(4,128)(2,1)S(1)}, u32[]{:S(2)}, u32[]{:S(2)}) collective-permute-start(bf16[4,7168]{1,0:T(4,128)(2,1)S(1)} %get-tuple-element.103), channel_id=1, source_target_pairs={{0,6},{1,7},{2,4},{3,5},{4,2},{5,3},{6,0},{7,1},{8,14},{9,15},{10,... | collective-permute-start | bytes 172040 | tf_op jit(solution)/shard_map/ppermute | solution.py:576
  104.3 2.6 %collective-permute-done.38.refs_7_ = bf16[4,7168]{1,0:T(4,128)(2,1)S(1)} collective-permute-done((bf16[4,7168]{1,0:T(4,128)(2,1)S(1)}, bf16[4,7168]{1,0:T(4,128)(2,1)S(1)}, u32[]{:S(2)}, u32[]{:S(2)}) %collective-permute-start.38) | collective-permute-done | bytes 57376 | tf_op jit(solution)/shard_map/ppermute | solution.py:576
  (113 shorter events, 38.9 us)
Async XLA Ops:
  0.0 7.5 %collective-permute-start.3 = (bf16[576,128]{1,0:T(8,128)(2,1)}, bf16[576,128]{1,0:T(8,128)(2,1)S(1)}, u32[]{:S(2)}, u32[]{:S(2)}) collective-permute-start(bf16[576,128]{1,0:T(8,128)(2,1)} %refs_0_.1), channel_id=1, source_target_pairs={{0,16},{1,17},{2,18},{3,19},{4,20},{5,21},{6,22},{7,23},{8,24},{9,... | collective-permute-start | bytes 442376 | tf_op jit(solution)/shard_map/ppermute | solution.py:576
  3.0 8.8 %collective-permute-start.7 = (bf16[32,576]{1,0:T(8,128)(2,1)}, bf16[32,576]{1,0:T(8,128)(2,1)S(1)}, u32[]{:S(2)}, u32[]{:S(2)}) collective-permute-start(bf16[32,576]{1,0:T(8,128)(2,1)} %bitcast.66), channel_id=1, source_target_pairs={{0,8},{1,9},{2,10},{3,11},{4,12},{5,13},{6,14},{7,15},{8,0},{9,1},... | collective-permute-start | bytes 110600 | tf_op jit(solution)/shard_map/ppermute | solution.py:576
  3.0 8.8 %collective-permute-start.4 = (bf16[576,128]{1,0:T(8,128)(2,1)}, bf16[576,128]{1,0:T(8,128)(2,1)S(1)}, u32[]{:S(2)}, u32[]{:S(2)}) collective-permute-start(bf16[576,128]{1,0:T(8,128)(2,1)} %refs_0_.1), channel_id=1, source_target_pairs={{0,8},{1,9},{2,10},{3,11},{4,12},{5,13},{6,14},{7,15},{8,0},{9,1},... | collective-permute-start | bytes 442376 | tf_op jit(solution)/shard_map/ppermute | solution.py:576
  15.7 5.5 %collective-permute-start.9 = (bf16[32,2048]{1,0:T(8,128)(2,1)S(1)}, bf16[32,2048]{1,0:T(8,128)(2,1)S(1)}, u32[]{:S(2)}, u32[]{:S(2)}) collective-permute-start(bf16[32,2048]{1,0:T(8,128)(2,1)S(1)} %get-tuple-element.58.refs_0_), channel_id=1, source_target_pairs={{0,16},{1,17},{2,18},{3,19},{4,20},{5,21},{6,22},{7,23},{8,24},{9,... | collective-permute-start | bytes 393224 | tf_op jit(solution)/shard_map/ppermute | solution.py:576
  24.5 10.8 %collective-permute-start.12 = (bf16[64,1792]{1,0:T(8,128)(2,1)S(1)}, bf16[64,1792]{1,0:T(8,128)(2,1)S(1)}, u32[]{:S(2)}, u32[]{:S(2)}) collective-permute-start(bf16[64,1792]{1,0:T(8,128)(2,1)S(1)} %get-tuple-element.61), channel_id=1, source_target_pairs={{0,1},{1,0},{2,3},{3,2},{4,5},{5,4},{6,7},{7,6},{8,9},{9,8},{10,11... | collective-permute-start | bytes 688136 | tf_op jit(solution)/shard_map/ppermute | solution.py:576
  27.0 12.6 %collective-permute-start = (bf16[4,1920]{1,0:T(4,128)(2,1)S(1)}, bf16[4,1920]{1,0:T(4,128)(2,1)S(1)}, u32[]{:S(2)}, u32[]{:S(2)}) collective-permute-start(bf16[4,1920]{1,0:T(4,128)(2,1)S(1)} %get-tuple-element.50), channel_id=1, source_target_pairs={{0,8},{1,9},{2,10},{3,11},{4,12},{5,13},{6,14},{7,15},{8,0},{9,1},... | collective-permute-start | bytes 46088 | tf_op jit(solution)/shard_map/ppermute | solution.py:576
  27.1 15.4 %collective-permute-start.1 = (bf16[4,1920]{1,0:T(4,128)(2,1)S(1)}, bf16[4,1920]{1,0:T(4,128)(2,1)S(1)}, u32[]{:S(2)}, u32[]{:S(2)}) collective-permute-start(bf16[4,1920]{1,0:T(4,128)(2,1)S(1)} %get-tuple-element.51), channel_id=1, source_target_pairs={{0,16},{1,17},{2,18},{3,19},{4,20},{5,21},{6,22},{7,23},{8,24},{9,... | collective-permute-start | bytes 46088 | tf_op jit(solution)/shard_map/ppermute | solution.py:576
  28.6 13.9 %collective-permute-start.2 = (bf16[4,1920]{1,0:T(4,128)(2,1)S(1)}, bf16[4,1920]{1,0:T(4,128)(2,1)S(1)}, u32[]{:S(2)}, u32[]{:S(2)}) collective-permute-start(bf16[4,1920]{1,0:T(4,128)(2,1)S(1)} %get-tuple-element.52), channel_id=1, source_target_pairs={{0,24},{1,25},{2,26},{3,27},{4,28},{5,29},{6,30},{7,31},{8,16},{9,... | collective-permute-start | bytes 46088 | tf_op jit(solution)/shard_map/ppermute | solution.py:576
  35.4 7.9 %collective-permute-start.13 = (bf16[16,1792]{1,0:T(8,128)(2,1)S(1)}, bf16[16,1792]{1,0:T(8,128)(2,1)S(1)}, u32[]{:S(2)}, u32[]{:S(2)}) collective-permute-start(bf16[16,1792]{1,0:T(8,128)(2,1)S(1)} %get-tuple-element.110), channel_id=1, source_target_pairs={{0,2},{1,3},{2,0},{3,1},{4,6},{5,7},{6,4},{7,5},{8,10},{9,11},{10,... | collective-permute-start | bytes 172040 | tf_op jit(solution)/shard_map/ppermute | solution.py:576
  37.0 6.5 %collective-permute-start.14 = (bf16[16,1792]{1,0:T(8,128)(2,1)S(1)}, bf16[16,1792]{1,0:T(8,128)(2,1)S(1)}, u32[]{:S(2)}, u32[]{:S(2)}) collective-permute-start(bf16[16,1792]{1,0:T(8,128)(2,1)S(1)} %get-tuple-element.109), channel_id=1, source_target_pairs={{0,4},{1,5},{2,6},{3,7},{4,0},{5,1},{6,2},{7,3},{8,12},{9,13},{10,... | collective-permute-start | bytes 172040 | tf_op jit(solution)/shard_map/ppermute | solution.py:576
  39.6 6.0 %collective-permute-start.15 = (bf16[16,1792]{1,0:T(8,128)(2,1)S(1)}, bf16[16,1792]{1,0:T(8,128)(2,1)S(1)}, u32[]{:S(2)}, u32[]{:S(2)}) collective-permute-start(bf16[16,1792]{1,0:T(8,128)(2,1)S(1)} %get-tuple-element.108), channel_id=1, source_target_pairs={{0,6},{1,7},{2,4},{3,5},{4,2},{5,3},{6,0},{7,1},{8,14},{9,15},{10,... | collective-permute-start | bytes 172040 | tf_op jit(solution)/shard_map/ppermute | solution.py:576
  45.7 7.2 %collective-permute-start.20 = (bf16[16,1920]{1,0:T(8,128)(2,1)S(1)}, bf16[16,1920]{1,0:T(8,128)(2,1)S(1)}, u32[]{:S(2)}, u32[]{:S(2)}) collective-permute-start(bf16[16,1920]{1,0:T(8,128)(2,1)S(1)} %get-tuple-element.67), channel_id=1, source_target_pairs={{0,4},{1,5},{2,6},{3,7},{4,0},{5,1},{6,2},{7,3},{8,12},{9,13},{10,... | collective-permute-start | bytes 184328 | tf_op jit(solution)/shard_map/ppermute | solution.py:576
  47.2 6.0 %collective-permute-start.21 = (bf16[16,1920]{1,0:T(8,128)(2,1)S(1)}, bf16[16,1920]{1,0:T(8,128)(2,1)S(1)}, u32[]{:S(2)}, u32[]{:S(2)}) collective-permute-start(bf16[16,1920]{1,0:T(8,128)(2,1)S(1)} %get-tuple-element.67), channel_id=1, source_target_pairs={{0,6},{1,7},{2,4},{3,5},{4,2},{5,3},{6,0},{7,1},{8,14},{9,15},{10,... | collective-permute-start | bytes 184328 | tf_op jit(solution)/shard_map/ppermute | solution.py:576
  54.9 6.1 %collective-permute-start.22 = (bf16[1,64,896]{2,1,0:T(8,128)(2,1)S(1)}, bf16[1,64,896]{2,1,0:T(8,128)(2,1)S(1)}, u32[]{:S(2)}, u32[]{:S(2)}) collective-permute-start(bf16[1,64,896]{2,1,0:T(8,128)(2,1)S(1)} %slice_bitcast_fusion.6), channel_id=1, source_target_pairs={{0,1},{1,0},{2,3},{3,2},{4,5},{5,4},{6,7},{7,6},{8,9},{9,8},{10,11... | collective-permute-start | bytes 344072 | tf_op jit(solution)/shard_map/ppermute | solution.py:576
  58.4 13.4 %collective-permute-start.28 = (bf16[2,64,1024]{2,1,0:T(8,128)(2,1)S(1)}, bf16[2,64,1024]{2,1,0:T(8,128)(2,1)S(1)}, u32[]{:S(2)}, u32[]{:S(2)}) collective-permute-start(bf16[2,64,1024]{2,1,0:T(8,128)(2,1)S(1)} %pad_maximum_fusion.1), channel_id=1, source_target_pairs={{0,1},{1,0},{2,3},{3,2},{4,5},{5,4},{6,7},{7,6},{8,9},{9,8},{10,11... | collective-permute-start | bytes 786440 | tf_op jit(solution)/shard_map/ppermute | solution.py:576
  61.0 10.7 %collective-permute-start.24 = (bf16[1,128,896]{2,1,0:T(8,128)(2,1)S(1)}, bf16[1,128,896]{2,1,0:T(8,128)(2,1)S(1)}, u32[]{:S(2)}, u32[]{:S(2)}) collective-permute-start(bf16[1,128,896]{2,1,0:T(8,128)(2,1)S(1)} %get-tuple-element.107), channel_id=1, source_target_pairs={{0,16},{1,17},{2,18},{3,19},{4,20},{5,21},{6,22},{7,23},{8,24},{9,... | collective-permute-start | bytes 688136 | tf_op jit(solution)/shard_map/ppermute | solution.py:576
  67.4 7.3 %collective-permute-start.23 = (bf16[1,128,896]{2,1,0:T(8,128)(2,1)S(1)}, bf16[1,128,896]{2,1,0:T(8,128)(2,1)S(1)}, u32[]{:S(2)}, u32[]{:S(2)}) collective-permute-start(bf16[1,128,896]{2,1,0:T(8,128)(2,1)S(1)} %get-tuple-element.107), channel_id=1, source_target_pairs={{0,8},{1,9},{2,10},{3,11},{4,12},{5,13},{6,14},{7,15},{8,0},{9,1},... | collective-permute-start | bytes 688136 | tf_op jit(solution)/shard_map/ppermute | solution.py:576
  80.0 21.0 %collective-permute-start.16 = (bf16[4,1792]{1,0:T(4,128)(2,1)S(1)}, bf16[4,1792]{1,0:T(4,128)(2,1)S(1)}, u32[]{:S(2)}, u32[]{:S(2)}) collective-permute-start(bf16[4,1792]{1,0:T(4,128)(2,1)S(1)} %get-tuple-element.64), channel_id=1, source_target_pairs={{0,8},{1,9},{2,10},{3,11},{4,12},{5,13},{6,14},{7,15},{8,0},{9,1},... | collective-permute-start | bytes 43016 | tf_op jit(solution)/shard_map/ppermute | solution.py:576
  80.4 22.4 %collective-permute-start.17 = (bf16[4,1792]{1,0:T(4,128)(2,1)S(1)}, bf16[4,1792]{1,0:T(4,128)(2,1)S(1)}, u32[]{:S(2)}, u32[]{:S(2)}) collective-permute-start(bf16[4,1792]{1,0:T(4,128)(2,1)S(1)} %get-tuple-element.65), channel_id=1, source_target_pairs={{0,16},{1,17},{2,18},{3,19},{4,20},{5,21},{6,22},{7,23},{8,24},{9,... | collective-permute-start | bytes 43016 | tf_op jit(solution)/shard_map/ppermute | solution.py:576
  82.0 20.9 %collective-permute-start.18 = (bf16[4,1792]{1,0:T(4,128)(2,1)S(1)}, bf16[4,1792]{1,0:T(4,128)(2,1)S(1)}, u32[]{:S(2)}, u32[]{:S(2)}) collective-permute-start(bf16[4,1792]{1,0:T(4,128)(2,1)S(1)} %get-tuple-element.66), channel_id=1, source_target_pairs={{0,24},{1,25},{2,26},{3,27},{4,28},{5,29},{6,30},{7,31},{8,16},{9,... | collective-permute-start | bytes 43016 | tf_op jit(solution)/shard_map/ppermute | solution.py:576
  83.9 7.6 %collective-permute-start.34 = (bf16[32,3584]{1,0:T(8,128)(2,1)S(1)}, bf16[32,3584]{1,0:T(8,128)(2,1)S(1)}, u32[]{:S(2)}, u32[]{:S(2)}) collective-permute-start(bf16[32,3584]{1,0:T(8,128)(2,1)S(1)} %slice.153), channel_id=1, source_target_pairs={{0,1},{1,0},{2,3},{3,2},{4,5},{5,4},{6,7},{7,6},{8,9},{9,8},{10,11... | collective-permute-start | bytes 688136 | tf_op jit(solution)/shard_map/ppermute | solution.py:576
  85.4 7.9 %collective-permute-start.31 = (bf16[32,3584]{1,0:T(8,128)(2,1)S(1)}, bf16[32,3584]{1,0:T(8,128)(2,1)S(1)}, u32[]{:S(2)}, u32[]{:S(2)}) collective-permute-start(bf16[32,3584]{1,0:T(8,128)(2,1)S(1)} %slice.154), channel_id=1, source_target_pairs={{0,16},{1,17},{2,18},{3,19},{4,20},{5,21},{6,22},{7,23},{8,24},{9,... | collective-permute-start | bytes 688136 | tf_op jit(solution)/shard_map/ppermute | solution.py:576
  98.7 5.7 %collective-permute-start.37 = (bf16[4,7168]{1,0:T(4,128)(2,1)S(1)}, bf16[4,7168]{1,0:T(4,128)(2,1)S(1)}, u32[]{:S(2)}, u32[]{:S(2)}) collective-permute-start(bf16[4,7168]{1,0:T(4,128)(2,1)S(1)} %get-tuple-element.104), channel_id=1, source_target_pairs={{0,4},{1,5},{2,6},{3,7},{4,0},{5,1},{6,2},{7,3},{8,12},{9,13},{10,... | collective-permute-start | bytes 172040 | tf_op jit(solution)/shard_map/ppermute | solution.py:576
  101.0 6.0 %collective-permute-start.38 = (bf16[4,7168]{1,0:T(4,128)(2,1)S(1)}, bf16[4,7168]{1,0:T(4,128)(2,1)S(1)}, u32[]{:S(2)}, u32[]{:S(2)}) collective-permute-start(bf16[4,7168]{1,0:T(4,128)(2,1)S(1)} %get-tuple-element.103), channel_id=1, source_target_pairs={{0,6},{1,7},{2,4},{3,5},{4,2},{5,3},{6,0},{7,1},{8,14},{9,15},{10,... | collective-permute-start | bytes 172040 | tf_op jit(solution)/shard_map/ppermute | solution.py:576
  (20 other events, 79.6 us)
